TPU v7x, 8 devices: a whole 2x2x1 slice. The times are simulated.
8 devices in a mesh: dp: 8 (over z, y, x, core).
Axes of the slice: x: 2, y: 2, z: 1, core: 2. Of those that a mesh axis runs over, the one named last changes fastest.
Arguments:
- tokens: bfloat16 [2048, 512], P('dp')
- w_one: bfloat16 [512, 2048], replicated
- w_two: bfloat16 [2048, 512], replicated
- wi_one: bfloat16 [512, 2048], replicated
- wi_two: bfloat16 [2048, 512], replicated
- item_table: bfloat16 [262144, 512], P('dp')
- cand_ids: int32 [16384], replicated
- log_q: float32 [16384], replicated
- targets: int32 [2048], P('dp')
Outputs:
- output 1: float32 [], replicated
- output 2: float32 [262144, 512], P('dp')
- output 3: float32 [512, 2048], replicated
- output 4: float32 [2048, 512], replicated
- output 5: float32 [512, 2048], replicated
- output 6: float32 [2048, 512], replicated
All inputs are finite; a program needn't handle non-finite values.
Results may differ from a plain program's by a relative error of at most 0.011808.
Values are sent between devices in bfloat16 or wider.
A program may use at most 1 GiB of HBM per device.

v0:
```python
import functools
import math
import jax
import jax.numpy as jnp
from jax import lax
from jax.experimental import pallas as pl
from jax.experimental.pallas import tpu as pltpu
from jax.sharding import PartitionSpec as P

SCORE_GAIN = 3.0
HIT_VALUE = -1e9
EXCLUDED = 3e38
NO_ROW = -1e9
CH = 512
BLK = 512
SUB = 8
TSUB = 4
PAIR = 2
WIN = 128
FB = 256
TB = 256
GELU_C = math.sqrt(2.0 / math.pi)
BF, F32 = jnp.bfloat16, jnp.float32
MESH = pl.DeviceIdType.MESH
VMEM_LIMIT = 60 * 1024 * 1024


def dot(a, b):
    return lax.dot_general(a, b, (((1,), (0,)), ((), ())), preferred_element_type=F32)


def dot_nt(a, b):
    return lax.dot_general(a, b, (((1,), (1,)), ((), ())), preferred_element_type=F32)


def gelu(x):
    half = 0.5 * x
    return half + half * jnp.tanh(x * (GELU_C + (GELU_C * 0.044715) * (x * x)))


def gelu_pair(x):
    sq = x * x
    th = jnp.tanh(x * (GELU_C + (GELU_C * 0.044715) * sq))
    half = 0.5 * x
    slope = (0.5 + 0.5 * th) + half * (1.0 - th * th) * (GELU_C + (3.0 * 0.044715 * GELU_C) * sq)
    return half + half * th, slope


def column(attr_ref, index, first, count):
    tiles = [attr_ref[first + i].T[:, index : index + 1] for i in range(count)]
    return jnp.concatenate(tiles, axis=0) if count > 1 else tiles[0]


def start_copies(nch_ref, copy):
    def step(i, carry):
        copy(i).start()
        return carry

    lax.fori_loop(0, nch_ref[0], step, 0)


def wait_copies(nch_ref, copy):
    def step(i, carry):
        copy(i).wait()
        return carry

    lax.fori_loop(0, nch_ref[0], step, 0)


def chunk_at(i):
    return pl.ds(pl.multiple_of(i * CH, CH), CH)


def gather_kernel(starts_ref, nch_ref, tbl_ref, attr_ref, rows_hbm, rows, keys, sem):
    step = pl.program_id(0)

    @pl.when(step == 0)
    def _():
        def prepare(i, carry):
            rows[chunk_at(i), :] = jnp.zeros((CH, rows.shape[1]), BF)
            for k in range(CH // WIN):
                at = pl.ds(pl.multiple_of(i * CH + k * WIN, WIN), WIN)
                key = attr_ref[i * (CH // WIN) + k].T[:, 0:1]
                keys[at, :] = jnp.broadcast_to(key, (WIN, WIN))
            return carry

        lax.fori_loop(0, nch_ref[0] + 1, prepare, 0)

    lanes = [(lax.broadcasted_iota(jnp.int32, (1, WIN), 1) + j).astype(F32) for j in range(0, BLK, WIN)]

    def picked(blk, part, at):
        key = keys[pl.ds(at, WIN), :] - (blk * BLK).astype(F32)
        pick = [jnp.where(key == lane, 1.0, 0.0).astype(BF) for lane in lanes]
        return dot(jnp.concatenate(pick, axis=1), tbl_ref[pl.ds(pl.multiple_of(part * BLK, BLK), BLK), :]).astype(BF)

    def some_blocks(i, carry):
        parts = [i * PAIR + k for k in range(PAIR)]
        blks = [step * SUB + part for part in parts]
        firsts = [(starts_ref[blk] >> 4) << 4 for blk in blks]
        gots = [picked(blk, part, pl.multiple_of(first, 16)) for blk, part, first in zip(blks, parts, firsts)]
        for blk, part, first, got in zip(blks, parts, firsts, gots):
            head = pl.ds(pl.multiple_of(first, 16), 16)
            rows[head, :] = rows[head, :] + got[:16]
            rows[pl.ds(pl.multiple_of(first + 16, 16), WIN - 16), :] = got[16:]

            def more(i, carry, blk=blk, part=part, first=first):
                at = pl.multiple_of(first + i * WIN, 16)
                rows[pl.ds(at, WIN), :] = picked(blk, part, at)
                return carry

            lax.fori_loop(1, (starts_ref[blk + 1] - first + (WIN - 1)) >> 7, more, 0)
        return carry

    lax.fori_loop(0, SUB // PAIR, some_blocks, 0)

    @pl.when(step == pl.num_programs(0) - 1)
    def _():
        copy = lambda i: pltpu.make_async_copy(rows.at[chunk_at(i), :], rows_hbm.at[chunk_at(i), :], sem)
        start_copies(nch_ref, copy)
        wait_copies(nch_ref, copy)


def stream(nch, body, ins, outs):
    specs = [[spec for spec, _ in part] for part in (ins, outs)]
    pltpu.emit_pipeline(body, grid=(nch,), in_specs=specs[0], out_specs=specs[1])(*[ref for _, ref in ins + outs])


def fwd_kernel(scale, nch_ref, tid_ref, h_ref, w1_ref, w2_ref, rows_hbm, attr_hbm, u_hbm, pre_hbm, z_hbm, stat_ref, m8, s8):
    m8[...] = jnp.full_like(m8, -EXCLUDED)
    s8[...] = jnp.zeros_like(s8)
    dim, ff, toks = rows_hbm.shape[1], w1_ref.shape[1], h_ref.shape[0]

    def body(rows_ref, attr_ref, u_ref, pre_ref, z_ref):
        rows = rows_ref[...]
        out = None
        for f in range(0, ff, FB):
            pre = dot(rows, w1_ref[:, f : f + FB])
            pre_ref[:, f : f + FB] = pre
            act = gelu(pre).astype(BF)
            part = dot(act, w2_ref[f : f + FB, :])
            out = part if out is None else out + part
        vec = out.astype(BF)
        u_ref[...] = vec
        loc = column(attr_ref, 0, 0, CH // WIN)
        off = column(attr_ref, 1, 0, CH // WIN)
        is_targ = column(attr_ref, 2, 0, CH // WIN) > 0.5
        for t in range(0, toks, TB):
            raw = dot_nt(vec, h_ref[t : t + TB, :]) * scale
            same = loc == tid_ref[:, t : t + TB]
            z = jnp.where(same, jnp.where(is_targ, raw, HIT_VALUE), raw - off)
            z_ref[:, t : t + TB] = z
            z3 = z.reshape(CH // 8, 8, TB)
            old = m8[:, t : t + TB]
            new = jnp.maximum(old, jnp.max(z3, axis=0))
            s8[:, t : t + TB] = s8[:, t : t + TB] * jnp.exp(old - new) + jnp.sum(jnp.exp(z3 - new[None]), axis=0)
            m8[:, t : t + TB] = new

    stream(nch_ref[0], body, [(chunk(dim), rows_hbm), (ATTR_CHUNK, attr_hbm)],
           [(chunk(dim), u_hbm), (chunk(ff), pre_hbm), (chunk(toks), z_hbm)])
    top = jnp.max(m8[...], axis=0, keepdims=True)
    stat_ref[0:1, :] = top
    stat_ref[1:2, :] = jnp.sum(s8[...] * jnp.exp(m8[...] - top), axis=0, keepdims=True)


def logit_back_kernel(scale, nch_ref, tid_ref, lse_ref, h_ref, z_hbm, u_hbm, attr_hbm, g_hbm, dht_ref):
    dht_ref[...] = jnp.zeros_like(dht_ref)
    dim, toks = u_hbm.shape[1], h_ref.shape[0]

    def body(z_ref, u_ref, attr_ref, g_ref):
        vec_t = u_ref[...].T
        loc = column(attr_ref, 0, 0, CH // WIN)
        is_targ = column(attr_ref, 2, 0, CH // WIN)
        shift = is_targ * (-1.0 / toks)
        grad = None
        log_toks = math.log(toks)
        for t in range(0, toks, TB):
            z = z_ref[:, t : t + TB]
            same = loc == tid_ref[:, t : t + TB]
            dz = (jnp.exp(z - (lse_ref[:, t : t + TB] + log_toks)) + jnp.where(same, shift, 0.0)).astype(BF)
            part = dot(dz, h_ref[t : t + TB, :])
            grad = part if grad is None else grad + part
            dht_ref[:dim, t : t + TB] += dot(vec_t, dz)
            zt = jnp.where(same, z * is_targ, 0.0)
            dht_ref[dim:, t : t + TB] += jnp.sum(zt.reshape(CH // 8, 8, TB), axis=0)
        g_ref[...] = (grad * scale).astype(BF)

    stream(nch_ref[0], body, [(chunk(toks), z_hbm), (chunk(dim), u_hbm), (ATTR_CHUNK, attr_hbm)], [(chunk(dim), g_hbm)])


def tower_back_kernel(nch_ref, w1_ref, w2_ref, g_hbm, rows_hbm, pre_hbm, drow_hbm, dw_ref):
    dw_ref[...] = jnp.zeros_like(dw_ref)
    dim, ff = w1_ref.shape

    def body(g_ref, rows_ref, pre_ref, drow_ref):
        g = g_ref[...]
        g_t, rows_t = g.T, rows_ref[...].T
        out = None
        for f in range(0, ff, FB):
            act, slope = gelu_pair(pre_ref[:, f : f + FB])
            q = (slope * dot_nt(g, w2_ref[f : f + FB, :])).astype(BF)
            dw_ref[dim:, f : f + FB] += dot(g_t, act.astype(BF))
            dw_ref[:dim, f : f + FB] += dot(rows_t, q)
            part = dot_nt(q, w1_ref[:, f : f + FB])
            out = part if out is None else out + part
        drow_ref[...] = out.astype(BF)

    stream(nch_ref[0], body, [(chunk(dim), g_hbm), (chunk(dim), rows_hbm), (chunk(ff), pre_hbm)], [(chunk(dim), drow_hbm)])


def query_back_kernel(scale, x_hbm, dht_hbm, w1_hbm, w2_hbm, part_hbm, dw1_ref, dw2t_ref, sum_ref,
                      x_ref, dht_ref, w1_ref, w2_ref, work, r0, r1, r2, load_sem, send_sem, recv_sem):
    me = lax.axis_index("dp")
    core, x, y = lax.rem(me, 2), lax.rem(lax.div(me, 2), 2), lax.div(me, 4)
    pair, x_peer, y_peer = me + 1 - 2 * core, me + 2 - 4 * x, me + 4 - 8 * y
    dim, ff = w1_ref.shape
    half = part_hbm.shape[0] // 2
    p1, p2, p3 = half // 2, half // 4, half // 8
    mine, other = core * half, (1 - core) * half

    barrier = pltpu.get_barrier_semaphore()
    for peer in (pair, x_peer, y_peer):
        pl.semaphore_signal(barrier, inc=1, device_id=(peer,), device_id_type=MESH)
    pl.semaphore_wait(barrier, 3)

    def rows(first, count):
        return pl.ds(pl.multiple_of(first, count), count)

    def send(k, src, dst, peer):
        copy = pltpu.make_async_remote_copy(
            src_ref=src, dst_ref=dst, send_sem=send_sem.at[k], recv_sem=recv_sem.at[k], device_id=(peer,), device_id_type=MESH)
        copy.start()
        return copy

    pair_copy = send(0, part_hbm.at[rows(other, half), :], r0, pair)
    loads = [(part_hbm.at[rows(mine, half), :], work), (x_hbm, x_ref), (dht_hbm.at[rows(0, dim), :], dht_ref), (w1_hbm, w1_ref), (w2_hbm, w2_ref)]
    loads = [pltpu.make_async_copy(src, dst, load_sem.at[i]) for i, (src, dst) in enumerate(loads)]
    for copy in loads:
        copy.start()
    dw1_ref[...] = jnp.zeros_like(dw1_ref)
    dw2t_ref[...] = jnp.zeros_like(dw2t_ref)
    for copy in loads:
        copy.wait()

    def unit(u, carry):
        tok = pl.ds(pl.multiple_of(lax.div(u, 2) * CH, CH), CH)
        first = lax.rem(u, 2) * (ff // 2)
        xs, grad_t = x_ref[tok, :], (dht_ref[:, tok] * scale).astype(BF)
        x_t, grad = xs.T, grad_t.T
        for f in range(0, ff // 2, FB):
            at = pl.ds(pl.multiple_of(first + f, FB), FB)
            act, slope = gelu_pair(dot(xs, w1_ref[:, at]))
            q = (slope * dot_nt(grad, w2_ref[at, :])).astype(BF)
            dw2t_ref[:, at] += dot(grad_t, act.astype(BF))
            dw1_ref[:, at] += dot(x_t, q)
        return carry

    pair_copy.wait()
    work[...] = work[...] + r0[...]
    step = [send(1, work.at[rows((1 - x) * p2, p2), :], r1.at[0], x_peer),
            send(2, work.at[rows(p1 + (1 - y) * p2, p2), :], r1.at[1], y_peer)]
    lax.fori_loop(0, 5, unit, 0)
    for copy in step:
        copy.wait()
    for at, k in ((rows(x * p2, p2), 0), (rows(p1 + y * p2, p2), 1)):
        work[at, :] = work[at, :] + r1[k]
    step = [send(3, work.at[rows(x * p2 + (1 - y) * p3, p3), :], r2.at[0], y_peer),
            send(4, work.at[rows(p1 + y * p2 + (1 - x) * p3, p3), :], r2.at[1], x_peer)]
    lax.fori_loop(5, 2 * (x_ref.shape[0] // CH), unit, 0)
    for copy in step:
        copy.wait()
    piece_a, piece_b = x * p2 + y * p3, p1 + y * p2 + x * p3
    step = []
    for k, piece, peer in ((0, piece_a, y_peer), (1, piece_b, x_peer)):
        at = rows(mine + piece, p3)
        sum_ref[at, :] = work[rows(piece, p3), :] + r2[k]
        step.append(send(5 + k, sum_ref.at[at, :], sum_ref.at[at, :], peer))
    for copy in step:
        copy.wait()
    at_a, at_b = rows(mine + x * p2, p2), rows(mine + p1 + y * p2, p2)
    step = [send(7, sum_ref.at[at_a, :], sum_ref.at[at_a, :], x_peer), send(8, sum_ref.at[at_b, :], sum_ref.at[at_b, :], y_peer)]
    last = [send(9, sum_ref.at[at_a, :], sum_ref.at[at_a, :], pair), send(10, sum_ref.at[at_b, :], sum_ref.at[at_b, :], pair)]
    for copy in step:
        copy.wait()
    at_a, at_b = rows(mine + (1 - x) * p2, p2), rows(mine + p1 + (1 - y) * p2, p2)
    last += [send(11, sum_ref.at[at_a, :], sum_ref.at[at_a, :], pair), send(12, sum_ref.at[at_b, :], sum_ref.at[at_b, :], pair)]
    for copy in last:
        copy.wait()


def table_kernel(starts_ref, nch_ref, attr_ref, drow_hbm, out_ref, drow, sem):
    step = pl.program_id(0)

    @pl.when(step == 0)
    def _():
        copy = lambda i: pltpu.make_async_copy(drow_hbm.at[chunk_at(i), :], drow.at[chunk_at(i), :], sem)
        start_copies(nch_ref, copy)
        drow[chunk_at(nch_ref[0]), :] = jnp.zeros((CH, drow.shape[1]), BF)
        wait_copies(nch_ref, copy)

    row = lax.broadcasted_iota(jnp.int32, (BLK, WIN), 0).astype(F32)

    def put(blk, tile):
        base = (blk * BLK).astype(F32)
        pick = [jnp.where(attr_ref[tile + k][0:1, :] - base == row, 1.0, 0.0).astype(BF) for k in range(2)]
        return dot(jnp.concatenate(pick, axis=1), drow[pl.ds(pl.multiple_of(tile * WIN, WIN), 2 * WIN), :])

    def some_blocks(i, carry):
        parts = [i * PAIR + k for k in range(PAIR)]
        firsts = [starts_ref[step * TSUB + part] >> 7 for part in parts]
        for part, first in zip(parts, firsts):
            out_ref[pl.ds(pl.multiple_of(part * BLK, BLK), BLK), :] = put(step * TSUB + part, first)
        for part, first in zip(parts, firsts):
            def more(i, carry, part=part, first=first):
                out_ref[pl.ds(pl.multiple_of(part * BLK, BLK), BLK), :] += put(step * TSUB + part, first + 2 * i)
                return carry

            hi = starts_ref[step * TSUB + part + 1]
            lax.fori_loop(1, (hi - first * WIN + (2 * WIN - 1)) >> 8, more, 0)
        return carry

    lax.fori_loop(0, TSUB // PAIR, some_blocks, 0)


def exchange(n, src_ref, all_ref, send_sem, recv_sem):
    me = lax.axis_index("dp")
    barrier = pltpu.get_barrier_semaphore()
    for k in range(1, n):
        pl.semaphore_signal(barrier, inc=1, device_id=(lax.rem(me + k, n),), device_id_type=MESH)
    pl.semaphore_wait(barrier, n - 1)
    copies = []
    for k in range(1, n):
        copies.append(pltpu.make_async_remote_copy(
            src_ref=src_ref, dst_ref=all_ref.at[me], send_sem=send_sem.at[k - 1], recv_sem=recv_sem.at[k - 1],
            device_id=(lax.rem(me + k, n),), device_id_type=MESH))
        copies[-1].start()
    all_ref[me] = src_ref[...]
    for copy in copies:
        copy.wait()


def targets_kernel(n, src_ref, out_ref, send_sem, recv_sem):
    exchange(n, src_ref, out_ref, send_sem, recv_sem)


def stats_kernel(n, src_ref, lse_ref, stats, send_sem, recv_sem):
    exchange(n, src_ref, stats, send_sem, recv_sem)
    top = stats[0, 0:1, :]
    for i in range(1, n):
        top = jnp.maximum(top, stats[i, 0:1, :])
    total = jnp.zeros_like(top)
    for i in range(n):
        total += stats[i, 1:2, :] * jnp.exp(stats[i, 0:1, :] - top)
    lse_ref[...] = top + jnp.log(total)


def share(kernel, ident, n, src, out, scratch=()):
    vmem = pl.BlockSpec(memory_space=pltpu.VMEM)
    return pl.pallas_call(
        functools.partial(kernel, n), out_shape=out, in_specs=[vmem], out_specs=vmem,
        scratch_shapes=[*scratch, pltpu.SemaphoreType.DMA((n - 1,)), pltpu.SemaphoreType.DMA((n - 1,))],
        compiler_params=pltpu.CompilerParams(collective_id=ident, has_side_effects=True),
    )(src)


def params(**kw):
    return pltpu.CompilerParams(vmem_limit_bytes=VMEM_LIMIT, dimension_semantics=("arbitrary",), **kw)


def cost(flops):
    return pl.CostEstimate(flops=flops, bytes_accessed=64 << 20, transcendentals=0)


def whole(shape):
    return pl.BlockSpec(shape, lambda i, *_: (0,) * len(shape))


def chunk(width):
    return pl.BlockSpec((CH, width), lambda i, *_: (i, 0))


ATTR_CHUNK = pl.BlockSpec((CH // WIN, 8, WIN), lambda i, *_: (i, 0, 0))


def sds(*shape, dtype=F32):
    return jax.ShapeDtypeStruct(shape, dtype)


def query_fwd(x, w_in, w_out):
    pre = jnp.dot(x, w_in, preferred_element_type=F32)
    hidden = jax.nn.gelu(pre).astype(BF)
    return jnp.dot(hidden, w_out, preferred_element_type=F32).astype(BF)


def solution(mesh):
    num_dev = mesh.shape["dp"]

    def local_step(tokens, w_one, w_two, wi_one, wi_two, table, cand_ids, log_q, targ_loc):
        dim = table.shape[1]
        ff = wi_one.shape[1]
        rows_loc = table.shape[0]
        toks = tokens.shape[0] * num_dev
        cands = cand_ids.shape[0]
        cap = cands + toks
        n_blk = rows_loc // BLK
        scale = SCORE_GAIN / math.sqrt(dim)
        base = lax.axis_index("dp") * rows_loc

        query_loc = query_fwd(tokens, w_one, w_two)
        query = lax.all_gather(query_loc, "dp", axis=0, tiled=True)
        x_all = lax.all_gather(tokens, "dp", axis=0, tiled=True)
        targ_all = share(targets_kernel, 0, num_dev, targ_loc[None, :], sds(num_dev, 1, targ_loc.shape[0], dtype=jnp.int32)).reshape(toks)

        ids = jnp.concatenate([cand_ids, targ_all]) - base
        kind = jnp.concatenate([jnp.zeros((cands,), jnp.int32), jnp.ones((toks,), jnp.int32)])
        key = jnp.where((ids >= 0) & (ids < rows_loc), 2 * ids + kind, 2 * rows_loc)
        offs = jnp.concatenate([log_q, jnp.full((toks,), EXCLUDED, F32)])
        bounds = jnp.arange(n_blk + 1, dtype=jnp.int32) * (2 * BLK)
        starts = jnp.sum((key[None, :] < bounds[:, None]).astype(jnp.int32), axis=1)
        nch = jnp.maximum(lax.div(starts[n_blk] + (CH - 1), CH), 1)
        key_s, offs_s = lax.sort((key, offs), num_keys=1, is_stable=False)
        repeat = jnp.concatenate([jnp.zeros((1,), bool), key_s[1:] == key_s[:-1]])
        used = (key_s < 2 * rows_loc) & ~repeat
        attr = jnp.stack([
            jnp.where(used, (key_s >> 1).astype(F32), NO_ROW),
            jnp.where(used, offs_s, EXCLUDED),
            jnp.where(used, (key_s & 1).astype(F32), 0.0),
        ])
        attr = jnp.pad(attr, ((0, 5), (0, 0)))
        pad = jnp.broadcast_to(jnp.array([NO_ROW, EXCLUDED, 0, 0, 0, 0, 0, 0], F32)[:, None], (8, CH))
        attr = jnp.concatenate([attr, pad], axis=1).reshape(8, -1, WIN).transpose(1, 0, 2)
        tid = (targ_all - base).astype(F32)[None, :]
        nch1 = nch[None]

        rows = pl.pallas_call(
            gather_kernel,
            grid_spec=pltpu.PrefetchScalarGridSpec(
                num_scalar_prefetch=2, grid=(n_blk // SUB,),
                in_specs=[pl.BlockSpec((SUB * BLK, dim), lambda i, *_: (i, 0)), whole(attr.shape)],
                out_specs=pl.BlockSpec(memory_space=pl.ANY),
                scratch_shapes=[pltpu.VMEM((cap + CH, dim), BF), pltpu.VMEM((cap + CH, WIN), F32), pltpu.SemaphoreType.DMA]),
            out_shape=sds(cap, dim, dtype=BF), compiler_params=params(), cost_estimate=cost(4 * rows_loc * WIN * dim), name="gather",
        )(starts, nch1, table, attr)

        def call(kernel, name, flops, ins, outs, scratch=()):
            spec = lambda shape, vmem: whole(shape) if vmem else pl.BlockSpec(memory_space=pl.ANY)
            return pl.pallas_call(
                kernel,
                grid_spec=pltpu.PrefetchScalarGridSpec(
                    num_scalar_prefetch=1, grid=(1,), in_specs=[spec(a.shape, v) for a, v in ins],
                    out_specs=[spec(o.shape, v) for o, v in outs], scratch_shapes=list(scratch)),
                out_shape=[o for o, _ in outs], compiler_params=params(), cost_estimate=cost(flops), name=name,
            )(nch1, *[a for a, _ in ins])

        bf_list, f_list = sds(cap, dim, dtype=BF), sds(cap, ff)
        vec, pre, z, stat = call(
            functools.partial(fwd_kernel, scale), "fwd", 6 * cap * dim * ff // 4,
            [(tid, True), (query, True), (wi_one, True), (wi_two, True), (rows, False), (attr, False)],
            [(bf_list, False), (f_list, False), (sds(cap, toks), False), (sds(2, toks), True)],
            [pltpu.VMEM((8, toks), F32), pltpu.VMEM((8, toks), F32)])

        stat, x_all = lax.optimization_barrier((stat, x_all))
        lse = share(stats_kernel, 1, num_dev, stat, sds(1, toks), [pltpu.VMEM((num_dev, 2, toks), F32)])

        g, dht_part = call(
            functools.partial(logit_back_kernel, scale), "logit_back", 4 * cap * dim * toks // 4,
            [(tid, True), (lse, True), (query, True), (z, False), (vec, False), (attr, False)],
            [(bf_list, False), (sds(dim + 8, toks), True)])

        dht = lax.psum(dht_part, "dp")
        drow, dwi_part = call(
            tower_back_kernel, "tower_back", 8 * cap * dim * ff // 4,
            [(wi_one, True), (wi_two, True), (g, False), (rows, False), (pre, False)],
            [(bf_list, False), (sds(2 * dim, ff), True)])

        d_table = pl.pallas_call(
            table_kernel,
            grid_spec=pltpu.PrefetchScalarGridSpec(
                num_scalar_prefetch=2, grid=(n_blk // TSUB,),
                in_specs=[whole(attr.shape), pl.BlockSpec(memory_space=pl.ANY)],
                out_specs=pl.BlockSpec((TSUB * BLK, dim), lambda i, *_: (i, 0)),
                scratch_shapes=[pltpu.VMEM((cap + CH, dim), BF), pltpu.SemaphoreType.DMA]),
            out_shape=sds(rows_loc, dim), compiler_params=params(), cost_estimate=cost(4 * rows_loc * WIN * dim), name="table",
        )(starts, nch1, attr, drow)

        any_spec, vmem = pl.BlockSpec(memory_space=pl.ANY), pl.BlockSpec(memory_space=pltpu.VMEM)
        dw_one, dw_two_t, dwi = pl.pallas_call(
            functools.partial(query_back_kernel, scale),
            in_specs=[any_spec] * 5, out_specs=[vmem] * 3,
            out_shape=[sds(dim, ff), sds(dim, ff), sds(2 * dim, ff)],
            scratch_shapes=[
                pltpu.VMEM((toks, dim), BF), pltpu.VMEM((dim, toks), F32), pltpu.VMEM((dim, ff), BF), pltpu.VMEM((ff, dim), BF),
                pltpu.VMEM((dim, ff), F32), pltpu.VMEM((dim, ff), F32),
                pltpu.VMEM((2, dim // 4, ff), F32), pltpu.VMEM((2, dim // 8, ff), F32),
                pltpu.SemaphoreType.DMA((5,)), pltpu.SemaphoreType.DMA((13,)), pltpu.SemaphoreType.DMA((13,))],
            compiler_params=pltpu.CompilerParams(vmem_limit_bytes=VMEM_LIMIT, collective_id=2, has_side_effects=True),
            cost_estimate=cost(8 * toks * dim * ff), name="query_back",
        )(x_all, dht, w_one, w_two, dwi_part)

        loss = (jnp.sum(lse) - jnp.sum(dht[dim:])) / toks
        dw_two, dwi_one, dwi_two = dw_two_t.T, dwi[:dim], dwi[dim:].T
        return loss, d_table, dw_one, dw_two, dwi_one, dwi_two

    return jax.shard_map(local_step, mesh=mesh, in_specs=(P("dp", None), P(), P(), P(), P(), P("dp", None), P(), P(), P("dp")), out_specs=(P(), P("dp", None), P(), P(), P(), P()), check_vma=False)
```

profile of v0, /device:TPU:0, one launch (start us, length us, event | category | flops | bytes accessed | tf_op | source)
XLA Modules:
  0.0 376.9 jit_solution(9862080074776139474)
XLA Ops:
  7.2 0.0 copy-start
  7.2 0.0 copy-start.3
  7.2 0.0 copy-start.2
  7.2 0.0 all-gather.3.cloned.1.call-start
  7.2 4.6 %convolution_convert_fusion = bf16[256,512]{1,0:T(8,128)(2,1)} fusion(bf16[2048,512]{1,0:T(8,128)(2,1)} %w2_hbm.1, bf16[256,512]{1,0:T(8,128)(2,1)} %param.10, bf16[512,2048]{1,0:T(8,128)(2,1)} %w1_hbm.1), kind=kOutput, calls=%fused_computation.11 | convolution fusion | flops 1078591488 | bytes 4718592 | tf_op jit(solution)/shard_map/dot_general | solution.py:391
  11.9 0.0 copy-start.5
  11.9 0.0 all-gather.3.cloned.1.call-update
  11.9 0.0 all-gather.5.cloned.1.call-start
  11.9 0.7 all-gather.5.cloned.1.call-update
  12.6 0.0 all-reduce.4.cloned.1.call-start
  12.7 7.8 %shard_map.145 = s32[8,1,256]{2,1,0:T(1,128)} custom-call(s32[1,256]{1,0:T(1,128)} %bitcast.25), custom_call_target="tpu_custom_call" | custom-call | tf_op jit(solution)/shard_map/pallas_call | solution.py:358
  20.6 0.0 copy-done.3
  20.6 1.3 subtract_convert_fusion
  21.9 0.0 copy-done
  21.9 0.0 copy-done.2
  21.9 0.7 add_select_fusion
  22.6 8.2 %sort.15 = (s32[18432]{0:T(1024)S(1)}, f32[18432]{0:T(1024)S(1)}) sort(s32[18432]{0:T(1024)S(1)} %add_select_fusion, f32[18432]{0:T(1024)S(1)} %concatenate.20), dimensions={0}, to_apply=%region_1.2 | sort | flops 276480 | bytes 294912 | tf_op jit(solution)/shard_map/sort | solution.py:420
  30.8 0.1 slice_compare_fusion
  30.9 0.1 convert_select_fusion.1
  31.0 0.2 select_maximum_fusion
  31.3 0.9 convert_reduce_fusion.starts_ref
  32.2 0.0 copy-start.4
  32.2 0.6 slice.18
  33.4 0.0 copy-done.5
  33.4 0.1 broadcast_in_dim.36
  33.5 0.9 maximum_bitcast_fusion.attr_ref.attr_hbm
  34.4 0.0 copy-done.4
  34.4 21.3 %gather.1.rows_hbm = bf16[18432,512]{1,0:T(8,128)(2,1)} custom-call(s32[65]{0:T(128)} %copy-done.4, s32[1]{0:T(128)} %bitcast.3.nch_ref, bf16[32768,512]{1,0:T(8,128)(2,1)} %tbl_ref.1, f32[148,8,128]{2,1,0:T(8,128)} %maximum_bitcast_fusion.attr_ref.attr_hbm), custom_call_target="tpu_custom_call" | custom-call | flops 8589934592 | bytes 67108864 | tf_op jit(solution)/shard_map/gather/pallas_call | solution.py:434
  55.7 0.0 all-gather.3.cloned.1.call-done.h_ref
  55.7 54.9 %fwd.1 = (bf16[18432,512]{1,0:T(8,128)(2,1)}, f32[18432,2048]{1,0:T(8,128)}, f32[18432,2048]{1,0:T(8,128)}, f32[2,2048]{1,0:T(2,128)}) custom-call(s32[1]{0:T(128)} %bitcast.3.nch_ref, f32[1,2048]{1,0:T(1,128)} %bitcast.23, bf16[2048,512]{1,0:T(8,128)(2,1)} %all-gather.3.cloned.1.call-done.h_ref, bf16[512,2048]{1,0:T(8,128)(2,1)} %w1_ref.3, ...), custom_call_target="tpu_custom_call" | custom-call | flops 28991029248 | bytes 67108864 | tf_op jit(solution)/shard_map/fwd/pallas_call | solution.py:446
  110.7 0.0 all-gather.5.cloned.1.call-done.x_hbm
  110.7 11.5 %shard_map.146.lse_ref = f32[1,2048]{1,0:T(1,128)} custom-call(f32[2,2048]{1,0:T(2,128)} %get-tuple-element.24.src_ref), custom_call_target="tpu_custom_call" | custom-call | tf_op jit(solution)/shard_map/pallas_call | solution.py:358
  122.1 32.9 %logit_back.1 = (bf16[18432,512]{1,0:T(8,128)(2,1)}, f32[520,2048]{1,0:T(8,128)}) custom-call(s32[1]{0:T(128)} %bitcast.3.nch_ref, f32[1,2048]{1,0:T(1,128)} %bitcast.24, f32[1,2048]{1,0:T(1,128)} %shard_map.146.lse_ref, bf16[2048,512]{1,0:T(8,128)(2,1)} %all-gather.3.cloned.1.call-done.h_ref, f32[18432,2048]{1,0:T(8,128)} %get-tuple-element.25.z_hbm, ...), custom_call_target="tpu_custom_call" | custom-call | flops 19327352832 | bytes 67108864 | tf_op jit(solution)/shard_map/logit_back/pallas_call | solution.py:446
  155.0 0.0 all-reduce.4.cloned.1.call-update
  155.1 0.0 copy-start.1
  155.1 59.4 %tower_back.1 = (bf16[18432,512]{1,0:T(8,128)(2,1)}, f32[1024,2048]{1,0:T(8,128)}) custom-call(s32[1]{0:T(128)} %bitcast.3.nch_ref, bf16[512,2048]{1,0:T(8,128)(2,1)} %w1_ref.3, bf16[2048,512]{1,0:T(8,128)(2,1)} %w2_ref.3, bf16[18432,512]{1,0:T(8,128)(2,1)} %get-tuple-element.28.g_hbm, bf16[18432,512]{1,0:T(8,128)(2,1)} %gather.1.rows_hbm, ...), custom_call_target="tpu_custom_call" | custom-call | flops 38654705664 | bytes 67108864 | tf_op jit(solution)/shard_map/tower_back/pallas_call | solution.py:446
  214.5 0.0 copy-done.1
  214.5 0.7 reduce_sum.28
  215.2 28.9 %table.1 = f32[32768,512]{1,0:T(8,128)} custom-call(s32[65]{0:T(128)} %copy-done.4, s32[1]{0:T(128)} %bitcast.3.nch_ref, f32[148,8,128]{2,1,0:T(8,128)} %maximum_bitcast_fusion.attr_ref.attr_hbm, bf16[18432,512]{1,0:T(8,128)(2,1)} %get-tuple-element.30.drow_hbm), custom_call_target="tpu_custom_call" | custom-call | flops 8589934592 | bytes 67108864 | tf_op jit(solution)/shard_map/table/pallas_call | solution.py:475
  244.0 0.0 all-reduce.4.cloned.1.call-done.dht_hbm
  244.1 99.0 %query_back.1 = (f32[512,2048]{1,0:T(8,128)}, f32[512,2048]{1,0:T(8,128)}, f32[1024,2048]{1,0:T(8,128)}) custom-call(bf16[2048,512]{1,0:T(8,128)(2,1)} %all-gather.5.cloned.1.call-done.x_hbm, f32[520,2048]{1,0:T(8,128)} %all-reduce.4.cloned.1.call-done.dht_hbm, bf16[512,2048]{1,0:T(8,128)(2,1)} %w1_hbm.1, bf16[2048,512]{1,0:T(8,128)(2,1)} %w2_hbm.1, ...), custom_call_target="tpu_custom_call" | custom-call | flops 17179869184 | bytes 67108864 | tf_op jit(solution)/shard_map/query_back/pallas_call | solution.py:486
  343.0 8.0 %slice_bitcast_fusion = (f32[2048,512]{0,1:T(8,128)}, f32[512,2048]{1,0:T(8,128)}) fusion(f32[1024,2048]{1,0:T(8,128)} %get-tuple-element.35), kind=kLoop, calls=%fused_computation.1 | loop fusion | bytes 16777216 | tf_op jit(solution)/shard_map/transpose | solution.py:500
  351.0 5.3 %copy.19 = f32[2048,512]{1,0:T(8,128)} copy(f32[2048,512]{0,1:T(8,128)} %get-tuple-element.48) | data formatting | bytes 8388608
  356.4 5.3 %copy.18 = f32[2048,512]{1,0:T(8,128)} copy(f32[2048,512]{0,1:T(8,128)} %bitcast.18) | data formatting | bytes 8388608
  361.7 1.5 slice_reduce_fusion
  364.5 4.7 %copy.22 = f32[512,2048]{1,0:T(8,128)} copy(f32[512,2048]{1,0:T(8,128)} %get-tuple-element.61) | data formatting | bytes 8388608
  (2 shorter events, 0.0 us)
Async XLA Ops:
  7.2 14.7 %copy-start = (s32[18432]{0:T(1024)S(1)}, s32[18432]{0:T(1024)}, u32[]{:S(2)}) copy-start(s32[18432]{0:T(1024)} %constant.24.clone.1) | copy-start | bytes 221188
  7.2 13.4 %copy-start.3 = (f32[16384]{0:T(1024)S(1)}, f32[16384]{0:T(1024)}, u32[]{:S(2)}) copy-start(f32[16384]{0:T(1024)} %param.17) | copy-start | bytes 196612
  7.2 14.7 %copy-start.2 = (s32[16384]{0:T(1024)S(1)}, s32[16384]{0:T(1024)}, u32[]{:S(2)}) copy-start(s32[16384]{0:T(1024)} %param.16) | copy-start | bytes 196612
  7.2 48.5 %all-gather.3.cloned.1.call-start = ((), (), s32[]{:S(2)}) async-start(), calls=%async_computation | async-start | bytes 2359296 | tf_op jit(solution)/shard_map/all_gather | solution.py:409
  11.9 21.6 %copy-start.5 = (f32[8]{0:T(128)S(1)}, f32[8]{0:T(128)}, u32[]{:S(2)}) copy-start(f32[8]{0:T(128)} %constant.56.clone) | copy-start | bytes 100
  11.9 98.8 %all-gather.5.cloned.1.call-start = ((), (), s32[]{:S(2)}) async-start(), calls=%async_computation.1 | async-start | bytes 2359296 | tf_op jit(solution)/shard_map/all_gather | solution.py:410
  12.6 231.4 %all-reduce.4.cloned.1.call-start = ((), (), s32[]{:S(2)}) async-start(), calls=%async_computation.2 | async-start | bytes 8519680 | tf_op jit(solution)/shard_map/psum | solution.py:469
  32.2 2.2 copy-start.4
  155.1 59.4 %copy-start.1 = (f32[1,2048]{1,0:T(1,128)S(1)}, f32[1,2048]{1,0:T(1,128)}, u32[]{:S(2)}) copy-start(f32[1,2048]{1,0:T(1,128)} %shard_map.146.lse_ref) | copy-start | bytes 24580
Sparse Core Ops, SparseCore 0:
  12.0 24.8 all-gather.2
  38.7 21.9 all-gather.4
  155.2 71.7 all-reduce.3
where the time goes:
time: 378 us; the launch traced here: 377 us
  Pallas kernels  316 us (84%)
  local copies, waits for them, and re-layouts  24 us (6%)
  between operations  17 us (4%)
  other arithmetic  14.6 us (4%)
  matrix products  4.61 us (1%)
    pallas_call x3, Pallas kernels, call(): pl.pallas_call(kernel, grid_spec=pltpu.PrefetchScalarGridSpec(num_scalar_...  147 us
    pallas_call x1, Pallas kernels, local_step(): pl.pallas_call(functools.partial(query_back_kernel, scale), in_specs=[any...  99 us
    pallas_call x1, Pallas kernels, local_step(): pl.pallas_call(table_kernel, grid_spec=pltpu.PrefetchScalarGridSpec(num_s...  28.9 us
    pallas_call x1, Pallas kernels, local_step(): pl.pallas_call(gather_kernel, grid_spec=pltpu.PrefetchScalarGridSpec(num_...  21.3 us
    pallas_call x2, Pallas kernels, share(): pl.pallas_call(functools.partial(kernel, n), out_shape=out, in_specs=[vme...  19.3 us
    unnamed x15, local copies, waits for them, and re-layouts  15.4 us
    sort x1, other arithmetic, local_step(): key_s, offs_s = lax.sort((key, offs), num_keys=1, is_stable=False)  8.22 us
    transpose x1, local copies, waits for them, and re-layouts, local_step(): dw_two, dwi_one, dwi_two = (dw_two_t.T, dwi[:dim], dwi[dim:].T)  7.97 us
  transfers between devices with their start and end apart: 3, of which 0 were waited for; matrix products, arithmetic and copies ran while one was open for 4% of the time, Pallas kernels for 46%

commit v1 on v0

--- a/solution.py
+++ b/solution.py
@@ -14,7 +14,6 @@
 CH = 512
 BLK = 512
 SUB = 8
-TSUB = 4
 PAIR = 2
 WIN = 128
 FB = 256
@@ -187,11 +186,51 @@
     stream(nch_ref[0], body, [(chunk(toks), z_hbm), (chunk(dim), u_hbm), (ATTR_CHUNK, attr_hbm)], [(chunk(dim), g_hbm)])
 
 
-def tower_back_kernel(nch_ref, w1_ref, w2_ref, g_hbm, rows_hbm, pre_hbm, drow_hbm, dw_ref):
+def tower_back_kernel(nch_ref, starts_ref, w1_ref, w2_ref, attr_ref, g_hbm, rows_hbm, pre_hbm, table_hbm, dw_ref, drow, ring, state, ring_sem):
     dw_ref[...] = jnp.zeros_like(dw_ref)
     dim, ff = w1_ref.shape
-
-    def body(g_ref, rows_ref, pre_ref, drow_ref):
+    n_blk = table_hbm.shape[0] // BLK
+    slots = ring.shape[0]
+    state[0] = 0
+    state[1] = 0
+
+    def clear(i, carry):
+        drow[chunk_at(i), :] = jnp.zeros((CH, dim), BF)
+        return carry
+
+    lax.fori_loop(0, nch_ref[0] + 1, clear, 0)
+    row = lax.broadcasted_iota(jnp.int32, (BLK, WIN), 0).astype(F32)
+
+    def put(blk, tile):
+        base = (blk * BLK).astype(F32)
+        pick = [jnp.where(attr_ref[tile + k][0:1, :] - base == row, 1.0, 0.0).astype(BF) for k in range(2)]
+        return dot(jnp.concatenate(pick, axis=1), drow[pl.ds(pl.multiple_of(tile * WIN, WIN), 2 * WIN), :])
+
+    def write(blk):
+        slot = lax.rem(blk, slots)
+        return pltpu.make_async_copy(ring.at[slot], table_hbm.at[pl.ds(pl.multiple_of(blk * BLK, BLK), BLK), :], ring_sem.at[slot])
+
+    def build(blk):
+        blks = [blk + k for k in range(PAIR)]
+
+        @pl.when(blk >= slots)
+        def _():
+            for one in blks:
+                write(one).wait()
+
+        firsts = [starts_ref[one] >> 7 for one in blks]
+        for one, first in zip(blks, firsts):
+            ring[lax.rem(one, slots)] = put(one, first)
+        for one, first in zip(blks, firsts):
+            def more(i, carry, one=one, first=first):
+                ring[lax.rem(one, slots)] += put(one, first + 2 * i)
+                return carry
+
+            lax.fori_loop(1, (starts_ref[one + 1] - first * WIN + (2 * WIN - 1)) >> 8, more, 0)
+            write(one).start()
+        return blk + PAIR
+
+    def body(g_ref, rows_ref, pre_ref):
         g = g_ref[...]
         g_t, rows_t = g.T, rows_ref[...].T
         out = None
@@ -202,13 +241,20 @@
             dw_ref[:dim, f : f + FB] += dot(rows_t, q)
             part = dot_nt(q, w1_ref[:, f : f + FB])
             out = part if out is None else out + part
-        drow_ref[...] = out.astype(BF)
-
-    stream(nch_ref[0], body, [(chunk(dim), g_hbm), (chunk(dim), rows_hbm), (chunk(ff), pre_hbm)], [(chunk(dim), drow_hbm)])
-
-
-def query_back_kernel(scale, x_hbm, dht_hbm, w1_hbm, w2_hbm, part_hbm, dw1_ref, dw2t_ref, sum_ref,
-                      x_ref, dht_ref, w1_ref, w2_ref, work, r0, r1, r2, load_sem, send_sem, recv_sem):
+        step = state[0]
+        drow[chunk_at(step), :] = out.astype(BF)
+        done = (step + 1) * CH
+        ready = lambda blk: (blk < n_blk) & (starts_ref[jnp.minimum(blk + PAIR, n_blk)] <= done)
+        state[1] = lax.while_loop(ready, build, state[1])
+        state[0] = step + 1
+
+    stream(nch_ref[0], body, [(chunk(dim), g_hbm), (chunk(dim), rows_hbm), (chunk(ff), pre_hbm)], [])
+    for blk in range(n_blk - slots, n_blk):
+        write(jnp.int32(blk)).wait()
+
+
+def query_back_kernel(scale, x_hbm, dht_hbm, w1_hbm, w2_hbm, part_hbm, dw1_hbm, dw2_hbm, dwi1_hbm, dwi2_hbm,
+                      dw1_ref, dw2t_ref, sum_ref, flip, x_ref, dht_ref, w1_ref, w2_ref, work, r0, r1, r2, load_sem, store_sem, send_sem, recv_sem):
     me = lax.axis_index("dp")
     core, x, y = lax.rem(me, 2), lax.rem(lax.div(me, 2), 2), lax.div(me, 4)
     pair, x_peer, y_peer = me + 1 - 2 * core, me + 2 - 4 * x, me + 4 - 8 * y
@@ -279,46 +325,24 @@
     at_a, at_b = rows(mine + x * p2, p2), rows(mine + p1 + y * p2, p2)
     step = [send(7, sum_ref.at[at_a, :], sum_ref.at[at_a, :], x_peer), send(8, sum_ref.at[at_b, :], sum_ref.at[at_b, :], y_peer)]
     last = [send(9, sum_ref.at[at_a, :], sum_ref.at[at_a, :], pair), send(10, sum_ref.at[at_b, :], sum_ref.at[at_b, :], pair)]
+    stores = [pltpu.make_async_copy(dw1_ref, dw1_hbm, store_sem.at[0]), pltpu.make_async_copy(flip.at[0], dw2_hbm, store_sem.at[1])]
+    stores[0].start()
+    for f in range(0, ff, FB):
+        flip[0, f : f + FB, :] = dw2t_ref[:, f : f + FB].T
+    stores[1].start()
     for copy in step:
         copy.wait()
     at_a, at_b = rows(mine + (1 - x) * p2, p2), rows(mine + p1 + (1 - y) * p2, p2)
     last += [send(11, sum_ref.at[at_a, :], sum_ref.at[at_a, :], pair), send(12, sum_ref.at[at_b, :], sum_ref.at[at_b, :], pair)]
     for copy in last:
         copy.wait()
-
-
-def table_kernel(starts_ref, nch_ref, attr_ref, drow_hbm, out_ref, drow, sem):
-    step = pl.program_id(0)
-
-    @pl.when(step == 0)
-    def _():
-        copy = lambda i: pltpu.make_async_copy(drow_hbm.at[chunk_at(i), :], drow.at[chunk_at(i), :], sem)
-        start_copies(nch_ref, copy)
-        drow[chunk_at(nch_ref[0]), :] = jnp.zeros((CH, drow.shape[1]), BF)
-        wait_copies(nch_ref, copy)
-
-    row = lax.broadcasted_iota(jnp.int32, (BLK, WIN), 0).astype(F32)
-
-    def put(blk, tile):
-        base = (blk * BLK).astype(F32)
-        pick = [jnp.where(attr_ref[tile + k][0:1, :] - base == row, 1.0, 0.0).astype(BF) for k in range(2)]
-        return dot(jnp.concatenate(pick, axis=1), drow[pl.ds(pl.multiple_of(tile * WIN, WIN), 2 * WIN), :])
-
-    def some_blocks(i, carry):
-        parts = [i * PAIR + k for k in range(PAIR)]
-        firsts = [starts_ref[step * TSUB + part] >> 7 for part in parts]
-        for part, first in zip(parts, firsts):
-            out_ref[pl.ds(pl.multiple_of(part * BLK, BLK), BLK), :] = put(step * TSUB + part, first)
-        for part, first in zip(parts, firsts):
-            def more(i, carry, part=part, first=first):
-                out_ref[pl.ds(pl.multiple_of(part * BLK, BLK), BLK), :] += put(step * TSUB + part, first + 2 * i)
-                return carry
-
-            hi = starts_ref[step * TSUB + part + 1]
-            lax.fori_loop(1, (hi - first * WIN + (2 * WIN - 1)) >> 8, more, 0)
-        return carry
-
-    lax.fori_loop(0, TSUB // PAIR, some_blocks, 0)
+    stores += [pltpu.make_async_copy(sum_ref.at[rows(0, dim), :], dwi1_hbm, store_sem.at[2]), pltpu.make_async_copy(flip.at[1], dwi2_hbm, store_sem.at[3])]
+    stores[2].start()
+    for f in range(0, ff, FB):
+        flip[1, f : f + FB, :] = sum_ref[dim:, f : f + FB].T
+    stores[3].start()
+    for copy in stores:
+        copy.wait()
 
 
 def exchange(n, src_ref, all_ref, send_sem, recv_sem):
@@ -442,13 +466,11 @@
         )(starts, nch1, table, attr)
 
         def call(kernel, name, flops, ins, outs, scratch=()):
-            spec = lambda shape, vmem: whole(shape) if vmem else pl.BlockSpec(memory_space=pl.ANY)
+            spec = lambda place: pl.BlockSpec(memory_space={True: pltpu.VMEM, False: pl.ANY, None: pltpu.SMEM}[place])
             return pl.pallas_call(
-                kernel,
-                grid_spec=pltpu.PrefetchScalarGridSpec(
-                    num_scalar_prefetch=1, grid=(1,), in_specs=[spec(a.shape, v) for a, v in ins],
-                    out_specs=[spec(o.shape, v) for o, v in outs], scratch_shapes=list(scratch)),
-                out_shape=[o for o, _ in outs], compiler_params=params(), cost_estimate=cost(flops), name=name,
+                kernel, in_specs=[spec(None)] + [spec(p) for _, p in ins], out_specs=[spec(p) for _, p in outs],
+                out_shape=[o for o, _ in outs], scratch_shapes=list(scratch),
+                compiler_params=pltpu.CompilerParams(vmem_limit_bytes=VMEM_LIMIT), cost_estimate=cost(flops), name=name,
             )(nch1, *[a for a, _ in ins])
 
         bf_list, f_list = sds(cap, dim, dtype=BF), sds(cap, ff)
@@ -467,37 +489,28 @@
             [(bf_list, False), (sds(dim + 8, toks), True)])
 
         dht = lax.psum(dht_part, "dp")
-        drow, dwi_part = call(
+        d_table, dwi_part = call(
             tower_back_kernel, "tower_back", 8 * cap * dim * ff // 4,
-            [(wi_one, True), (wi_two, True), (g, False), (rows, False), (pre, False)],
-            [(bf_list, False), (sds(2 * dim, ff), True)])
-
-        d_table = pl.pallas_call(
-            table_kernel,
-            grid_spec=pltpu.PrefetchScalarGridSpec(
-                num_scalar_prefetch=2, grid=(n_blk // TSUB,),
-                in_specs=[whole(attr.shape), pl.BlockSpec(memory_space=pl.ANY)],
-                out_specs=pl.BlockSpec((TSUB * BLK, dim), lambda i, *_: (i, 0)),
-                scratch_shapes=[pltpu.VMEM((cap + CH, dim), BF), pltpu.SemaphoreType.DMA]),
-            out_shape=sds(rows_loc, dim), compiler_params=params(), cost_estimate=cost(4 * rows_loc * WIN * dim), name="table",
-        )(starts, nch1, attr, drow)
-
-        any_spec, vmem = pl.BlockSpec(memory_space=pl.ANY), pl.BlockSpec(memory_space=pltpu.VMEM)
-        dw_one, dw_two_t, dwi = pl.pallas_call(
+            [(starts, None), (wi_one, True), (wi_two, True), (attr, True), (g, False), (rows, False), (pre, False)],
+            [(sds(rows_loc, dim), False), (sds(2 * dim, ff), True)],
+            [pltpu.VMEM((cap + CH, dim), BF), pltpu.VMEM((4, BLK, dim), F32), pltpu.SMEM((2,), jnp.int32), pltpu.SemaphoreType.DMA((4,))])
+
+        any_spec = pl.BlockSpec(memory_space=pl.ANY)
+        dw_one, dw_two, dwi_one, dwi_two = pl.pallas_call(
             functools.partial(query_back_kernel, scale),
-            in_specs=[any_spec] * 5, out_specs=[vmem] * 3,
-            out_shape=[sds(dim, ff), sds(dim, ff), sds(2 * dim, ff)],
+            in_specs=[any_spec] * 5, out_specs=[any_spec] * 4,
+            out_shape=[sds(dim, ff), sds(ff, dim), sds(dim, ff), sds(ff, dim)],
             scratch_shapes=[
+                pltpu.VMEM((dim, ff), F32), pltpu.VMEM((dim, ff), F32), pltpu.VMEM((2 * dim, ff), F32), pltpu.VMEM((2, ff, dim), F32),
                 pltpu.VMEM((toks, dim), BF), pltpu.VMEM((dim, toks), F32), pltpu.VMEM((dim, ff), BF), pltpu.VMEM((ff, dim), BF),
                 pltpu.VMEM((dim, ff), F32), pltpu.VMEM((dim, ff), F32),
                 pltpu.VMEM((2, dim // 4, ff), F32), pltpu.VMEM((2, dim // 8, ff), F32),
-                pltpu.SemaphoreType.DMA((5,)), pltpu.SemaphoreType.DMA((13,)), pltpu.SemaphoreType.DMA((13,))],
+                pltpu.SemaphoreType.DMA((5,)), pltpu.SemaphoreType.DMA((4,)), pltpu.SemaphoreType.DMA((13,)), pltpu.SemaphoreType.DMA((13,))],
             compiler_params=pltpu.CompilerParams(vmem_limit_bytes=VMEM_LIMIT, collective_id=2, has_side_effects=True),
             cost_estimate=cost(8 * toks * dim * ff), name="query_back",
         )(x_all, dht, w_one, w_two, dwi_part)
 
         loss = (jnp.sum(lse) - jnp.sum(dht[dim:])) / toks
-        dw_two, dwi_one, dwi_two = dw_two_t.T, dwi[:dim], dwi[dim:].T
         return loss, d_table, dw_one, dw_two, dwi_one, dwi_two
 
     return jax.shard_map(local_step, mesh=mesh, in_specs=(P("dp", None), P(), P(), P(), P(), P("dp", None), P(), P(), P("dp")), out_specs=(P(), P("dp", None), P(), P(), P(), P()), check_vma=False)

time: 378 us -> 362 us (0.958)
  local copies, waits for them, and re-layouts: 24 us -> 15.6 us
  Pallas kernels: 316 us -> 309 us
    pallas_call x1, Pallas kernels: 99 us -> 88.3 us  [local_step(): pl.pallas_call(functools.partial(query_back_kernel, scale), in_specs=[any...]
    pallas_call x4 -> x3, Pallas kernels: 176 us -> 185 us  [call(): pl.pallas_call(kernel, in_specs=[spec(None)] + [spec(p) for _, p in ins],...]
    transpose x1 -> x0, local copies, waits for them, and re-layouts: 7.97 us -> none  [local_step(): dw_two, dwi_one, dwi_two = (dw_two_t.T, dwi[:dim], dwi[dim:].T)]
    pallas_call x2, Pallas kernels: 19.3 us -> 14.1 us  [share(): pl.pallas_call(functools.partial(kernel, n), out_shape=out, in_specs=[vme...]
    unnamed x15 -> x22, local copies, waits for them, and re-layouts: 15.4 us -> 15 us
  transfers between devices with their start and end apart: 3 -> 3, of which waited for: 0 -> 0; matrix products, arithmetic and copies ran while one was open for 4% -> 4% of each run, Pallas kernels for 46% -> 49%
where the time goes in v1:
time: 362 us
  Pallas kernels  309 us (85%)
  between operations  17 us (5%)
  local copies, waits for them, and re-layouts  15.6 us (4%)
  other arithmetic  14.5 us (4%)
  matrix products  4.61 us (1%)
    pallas_call x3, Pallas kernels, call(): pl.pallas_call(kernel, in_specs=[spec(None)] + [spec(p) for _, p in ins],...  185 us
    pallas_call x1, Pallas kernels, local_step(): pl.pallas_call(functools.partial(query_back_kernel, scale), in_specs=[any...  88.3 us
    pallas_call x1, Pallas kernels, local_step(): pl.pallas_call(gather_kernel, grid_spec=pltpu.PrefetchScalarGridSpec(num_...  21.8 us
    unnamed x22, local copies, waits for them, and re-layouts  15 us
    pallas_call x2, Pallas kernels, share(): pl.pallas_call(functools.partial(kernel, n), out_shape=out, in_specs=[vme...  14.1 us
    sort x1, other arithmetic, local_step(): key_s, offs_s = lax.sort((key, offs), num_keys=1, is_stable=False)  8.22 us
  transfers between devices with their start and end apart: 3, of which 0 were waited for; matrix products, arithmetic and copies ran while one was open for 4% of the time, Pallas kernels for 49%

profile of v1, /device:TPU:0, one launch (start us, length us, event | category | flops | bytes accessed | tf_op | source)
XLA Modules:
  0.0 361.6 jit_solution(3628032485462339157)
XLA Ops:
  7.2 0.0 copy-start.3
  7.2 0.0 copy-start.6
  7.2 0.0 copy-start.5
  7.2 0.0 all-gather.3.cloned.1.call-start
  7.2 4.6 %convolution_convert_fusion = bf16[256,512]{1,0:T(8,128)(2,1)} fusion(bf16[2048,512]{1,0:T(8,128)(2,1)} %w2_hbm.1, bf16[256,512]{1,0:T(8,128)(2,1)} %param.10, bf16[512,2048]{1,0:T(8,128)(2,1)} %w1_hbm.1), kind=kOutput, calls=%fused_computation.10 | convolution fusion | flops 1078591488 | bytes 4718592 | tf_op jit(solution)/shard_map/dot_general | solution.py:415
  11.9 0.0 copy-start.8
  11.9 0.0 all-gather.3.cloned.1.call-update
  11.9 0.0 all-gather.5.cloned.1.call-start
  11.9 0.7 all-gather.5.cloned.1.call-update
  12.6 0.0 all-reduce.4.cloned.1.call-start
  12.7 7.8 %shard_map.145 = s32[8,1,256]{2,1,0:T(1,128)} custom-call(s32[1,256]{1,0:T(1,128)} %bitcast.21), custom_call_target="tpu_custom_call" | custom-call | tf_op jit(solution)/shard_map/pallas_call | solution.py:382
  20.6 0.0 copy-done.6
  20.6 1.3 subtract_convert_fusion
  21.9 0.0 copy-done.3
  21.9 0.0 copy-done.5
  21.9 0.7 add_select_fusion
  22.6 8.2 %sort.15 = (s32[18432]{0:T(1024)S(1)}, f32[18432]{0:T(1024)S(1)}) sort(s32[18432]{0:T(1024)S(1)} %add_select_fusion, f32[18432]{0:T(1024)S(1)} %concatenate.20), dimensions={0}, to_apply=%region_1.2 | sort | flops 276480 | bytes 294912 | tf_op jit(solution)/shard_map/sort | solution.py:444
  30.8 0.1 slice_compare_fusion
  30.9 0.1 convert_select_fusion.1
  31.0 0.2 select_maximum_fusion
  31.3 0.9 convert_reduce_fusion.starts_ref
  32.2 0.0 copy-start.7
  32.2 0.6 slice.12
  33.4 0.0 copy-done.8
  33.4 0.1 broadcast_in_dim.36
  33.5 0.9 maximum_bitcast_fusion.attr_ref.attr_hbm
  34.4 0.0 copy-done.7
  34.4 21.8 %gather.1.rows_hbm = bf16[18432,512]{1,0:T(8,128)(2,1)} custom-call(s32[65]{0:T(128)} %copy-done.7, s32[1]{0:T(128)} %bitcast.3.nch_ref, bf16[32768,512]{1,0:T(8,128)(2,1)} %tbl_ref.1, f32[148,8,128]{2,1,0:T(8,128)} %maximum_bitcast_fusion.attr_ref.attr_hbm), custom_call_target="tpu_custom_call" | custom-call | flops 8589934592 | bytes 67108864 | tf_op jit(solution)/shard_map/gather/pallas_call | solution.py:458
  56.2 0.0 all-gather.3.cloned.1.call-done.h_ref
  56.2 60.0 %fwd.1 = (bf16[18432,512]{1,0:T(8,128)(2,1)}, f32[18432,2048]{1,0:T(8,128)}, f32[18432,2048]{1,0:T(8,128)}, f32[2,2048]{1,0:T(2,128)}) custom-call(s32[1]{0:T(128)} %bitcast.3.nch_ref, f32[1,2048]{1,0:T(1,128)} %bitcast.19, bf16[2048,512]{1,0:T(8,128)(2,1)} %all-gather.3.cloned.1.call-done.h_ref, bf16[512,2048]{1,0:T(8,128)(2,1)} %w1_ref.3, ...), custom_call_target="tpu_custom_call" | custom-call | flops 28991029248 | bytes 67108864 | tf_op jit(solution)/shard_map/fwd/pallas_call | solution.py:470
  116.2 0.0 all-gather.5.cloned.1.call-done.x_hbm
  116.2 6.3 %shard_map.146.lse_ref = f32[1,2048]{1,0:T(1,128)} custom-call(f32[2,2048]{1,0:T(2,128)} %get-tuple-element.25.src_ref), custom_call_target="tpu_custom_call" | custom-call | tf_op jit(solution)/shard_map/pallas_call | solution.py:382
  122.5 35.7 %logit_back.1 = (bf16[18432,512]{1,0:T(8,128)(2,1)}, f32[520,2048]{1,0:T(8,128)}) custom-call(s32[1]{0:T(128)} %bitcast.3.nch_ref, f32[1,2048]{1,0:T(1,128)} %bitcast.20, f32[1,2048]{1,0:T(1,128)} %shard_map.146.lse_ref, bf16[2048,512]{1,0:T(8,128)(2,1)} %all-gather.3.cloned.1.call-done.h_ref, f32[18432,2048]{1,0:T(8,128)} %get-tuple-element.26.z_hbm, ...), custom_call_target="tpu_custom_call" | custom-call | flops 19327352832 | bytes 67108864 | tf_op jit(solution)/shard_map/logit_back/pallas_call | solution.py:470
  158.2 0.0 all-reduce.4.cloned.1.call-update
  158.2 0.7 copy-done.4
  158.9 0.6 reduce_sum.28
  159.5 89.1 %tower_back.1 = (f32[32768,512]{1,0:T(8,128)}, f32[1024,2048]{1,0:T(8,128)}) custom-call(s32[1]{0:T(128)} %bitcast.3.nch_ref, s32[65]{0:T(128)} %copy-done.7, bf16[512,2048]{1,0:T(8,128)(2,1)} %w1_ref.3, bf16[2048,512]{1,0:T(8,128)(2,1)} %w2_ref.3, f32[148,8,128]{2,1,0:T(8,128)} %maximum_bitcast_fusion.attr_ref.attr_hbm, ...), custom_call_target="tpu_custom_call" | custom-call | flops 38654705664 | bytes 67108864 | tf_op jit(solution)/shard_map/tower_back/pallas_call | solution.py:470
  248.6 0.0 all-reduce.4.cloned.1.call-done.dht_hbm
  248.7 88.3 %query_back.1 = (f32[512,2048]{1,0:T(8,128)}, f32[2048,512]{1,0:T(8,128)}, f32[512,2048]{1,0:T(8,128)}, f32[2048,512]{1,0:T(8,128)}) custom-call(bf16[2048,512]{1,0:T(8,128)(2,1)} %all-gather.5.cloned.1.call-done.x_hbm, f32[520,2048]{1,0:T(8,128)} %all-reduce.4.cloned.1.call-done.dht_hbm, bf16[512,2048]{1,0:T(8,128)(2,1)} %w1_hbm.1, ...), custom_call_target="tpu_custom_call" | custom-call | flops 17179869184 | bytes 67108864 | tf_op jit(solution)/shard_map/query_back/pallas_call | solution.py:499
  336.9 1.5 slice_reduce_fusion
  339.7 0.0 copy-start.2
  339.7 4.8 %copy.21 = f32[512,2048]{1,0:T(8,128)} copy(f32[512,2048]{1,0:T(8,128)} %get-tuple-element.49) | data formatting | bytes 8388608
  344.6 0.0 copy-done.2
  344.6 2.1 copy.22
  346.7 1.6 copy-done.1
  348.3 2.1 copy.23
  350.4 1.6 copy-done
  352.0 2.0 copy.24
  (5 shorter events, 0.0 us)
Async XLA Ops:
  7.2 14.7 %copy-start.3 = (s32[18432]{0:T(1024)S(1)}, s32[18432]{0:T(1024)}, u32[]{:S(2)}) copy-start(s32[18432]{0:T(1024)} %constant.24.clone.1) | copy-start | bytes 221188
  7.2 13.4 %copy-start.6 = (f32[16384]{0:T(1024)S(1)}, f32[16384]{0:T(1024)}, u32[]{:S(2)}) copy-start(f32[16384]{0:T(1024)} %param.17) | copy-start | bytes 196612
  7.2 14.7 %copy-start.5 = (s32[16384]{0:T(1024)S(1)}, s32[16384]{0:T(1024)}, u32[]{:S(2)}) copy-start(s32[16384]{0:T(1024)} %param.16) | copy-start | bytes 196612
  7.2 49.0 %all-gather.3.cloned.1.call-start = ((), (), s32[]{:S(2)}) async-start(), calls=%async_computation | async-start | bytes 2359296 | tf_op jit(solution)/shard_map/all_gather | solution.py:433
  11.9 21.6 %copy-start.8 = (f32[8]{0:T(128)S(1)}, f32[8]{0:T(128)}, u32[]{:S(2)}) copy-start(f32[8]{0:T(128)} %constant.56.clone) | copy-start | bytes 100
  11.9 104.3 %all-gather.5.cloned.1.call-start = ((), (), s32[]{:S(2)}) async-start(), calls=%async_computation.1 | async-start | bytes 2359296 | tf_op jit(solution)/shard_map/all_gather | solution.py:434
  12.6 236.0 %all-reduce.4.cloned.1.call-start = ((), (), s32[]{:S(2)}) async-start(), calls=%async_computation.2 | async-start | bytes 8519680 | tf_op jit(solution)/shard_map/psum | solution.py:491
  32.2 2.2 copy-start.7
  158.2 0.7 copy-start.4
  339.7 4.9 %copy-start.2 = (f32[2048,512]{1,0:T(8,128)S(1)}, f32[2048,512]{1,0:T(8,128)}, u32[]{:S(2)}) copy-start(f32[2048,512]{1,0:T(8,128)} %get-tuple-element.50) | copy-start | bytes 12582916
  344.6 3.7 %copy-start.1 = (f32[512,2048]{1,0:T(8,128)S(1)}, f32[512,2048]{1,0:T(8,128)}, u32[]{:S(2)}) copy-start(f32[512,2048]{1,0:T(8,128)} %get-tuple-element.51) | copy-start | bytes 12582916
  348.3 3.7 %copy-start = (f32[2048,512]{1,0:T(8,128)S(1)}, f32[2048,512]{1,0:T(8,128)}, u32[]{:S(2)}) copy-start(f32[2048,512]{1,0:T(8,128)} %get-tuple-element.52) | copy-start | bytes 12582916
Sparse Core Ops, SparseCore 0:
  12.0 24.8 all-gather.2
  38.7 21.9 all-gather.4
  158.4 68.8 all-reduce.3

commit v2 on v1

--- a/solution.py
+++ b/solution.py
@@ -13,6 +13,7 @@
 NO_ROW = -1e9
 CH = 512
 BLK = 512
+TCH = 512
 SUB = 8
 PAIR = 2
 WIN = 128
@@ -254,14 +255,15 @@
 
 
 def query_back_kernel(scale, x_hbm, dht_hbm, w1_hbm, w2_hbm, part_hbm, dw1_hbm, dw2_hbm, dwi1_hbm, dwi2_hbm,
-                      dw1_ref, dw2t_ref, sum_ref, flip, x_ref, dht_ref, w1_ref, w2_ref, work, r0, r1, r2, load_sem, store_sem, send_sem, recv_sem):
+                      dw1_ref, dw2t_ref, sum_ref, flip, x_ref, x_t, dht_ref, grad_t, grad, w1_ref, w2_ref, work, r0, r1, r2,
+                      load_sem, store_sem, send_sem, recv_sem):
     me = lax.axis_index("dp")
     core, x, y = lax.rem(me, 2), lax.rem(lax.div(me, 2), 2), lax.div(me, 4)
     pair, x_peer, y_peer = me + 1 - 2 * core, me + 2 - 4 * x, me + 4 - 8 * y
     dim, ff = w1_ref.shape
-    half = part_hbm.shape[0] // 2
+    toks = x_ref.shape[0]
+    half = dim // 2
     p1, p2, p3 = half // 2, half // 4, half // 8
-    mine, other = core * half, (1 - core) * half
 
     barrier = pltpu.get_barrier_semaphore()
     for peer in (pair, x_peer, y_peer):
@@ -271,78 +273,120 @@
     def rows(first, count):
         return pl.ds(pl.multiple_of(first, count), count)
 
-    def send(k, src, dst, peer):
+    def send(j, k, src, dst, peer):
+        sems = send_sem.at[13 * j + k], recv_sem.at[13 * j + k]
         copy = pltpu.make_async_remote_copy(
-            src_ref=src, dst_ref=dst, send_sem=send_sem.at[k], recv_sem=recv_sem.at[k], device_id=(peer,), device_id_type=MESH)
+            src_ref=src, dst_ref=dst, send_sem=sems[0], recv_sem=sems[1], device_id=(peer,), device_id_type=MESH)
         copy.start()
         return copy
 
-    pair_copy = send(0, part_hbm.at[rows(other, half), :], r0, pair)
-    loads = [(part_hbm.at[rows(mine, half), :], work), (x_hbm, x_ref), (dht_hbm.at[rows(0, dim), :], dht_ref), (w1_hbm, w1_ref), (w2_hbm, w2_ref)]
+    def wait(copies):
+        for copy in copies:
+            copy.wait()
+
+    def mine(j):
+        return j * dim + core * half
+
+    def stage0(j):
+        return [send(j, 0, part_hbm.at[rows(j * dim + (1 - core) * half, half), :], r0.at[j], pair)]
+
+    def stage1(j):
+        work[j] = work[j] + r0[j]
+        return [send(j, 1, work.at[j, rows((1 - x) * p2, p2), :], r1.at[j, 0], x_peer),
+                send(j, 2, work.at[j, rows(p1 + (1 - y) * p2, p2), :], r1.at[j, 1], y_peer)]
+
+    def stage2(j):
+        for at, k in ((rows(x * p2, p2), 0), (rows(p1 + y * p2, p2), 1)):
+            work[j, at, :] = work[j, at, :] + r1[j, k]
+        return [send(j, 3, work.at[j, rows(x * p2 + (1 - y) * p3, p3), :], r2.at[j, 0], y_peer),
+                send(j, 4, work.at[j, rows(p1 + y * p2 + (1 - x) * p3, p3), :], r2.at[j, 1], x_peer)]
+
+    def share_rows(j, k, first, count, peer):
+        at = rows(mine(j) + first, count)
+        return send(j, k, sum_ref.at[at, :], sum_ref.at[at, :], peer)
+
+    def stage3(j):
+        piece_a, piece_b = x * p2 + y * p3, p1 + y * p2 + x * p3
+        for k, piece in ((0, piece_a), (1, piece_b)):
+            sum_ref[rows(mine(j) + piece, p3), :] = work[j, rows(piece, p3), :] + r2[j, k]
+        return [share_rows(j, 5, piece_a, p3, y_peer), share_rows(j, 6, piece_b, p3, x_peer)]
+
+    def stage4(j):
+        step = [share_rows(j, 7, x * p2, p2, x_peer), share_rows(j, 8, p1 + y * p2, p2, y_peer)]
+        return step, [share_rows(j, 9, x * p2, p2, pair), share_rows(j, 10, p1 + y * p2, p2, pair)]
+
+    def stage5(j):
+        return [share_rows(j, 11, (1 - x) * p2, p2, pair), share_rows(j, 12, p1 + (1 - y) * p2, p2, pair)]
+
+    step = [stage0(0), stage0(1)]
+    loads = [(part_hbm.at[rows(mine(j), half), :], work.at[j]) for j in range(2)]
+    loads += [(x_hbm, x_ref), (dht_hbm.at[rows(0, dim), :], dht_ref), (w1_hbm, w1_ref), (w2_hbm, w2_ref)]
     loads = [pltpu.make_async_copy(src, dst, load_sem.at[i]) for i, (src, dst) in enumerate(loads)]
     for copy in loads:
         copy.start()
     dw1_ref[...] = jnp.zeros_like(dw1_ref)
     dw2t_ref[...] = jnp.zeros_like(dw2t_ref)
-    for copy in loads:
-        copy.wait()
+    wait(loads)
+
+    def turn(i, carry):
+        tok = pl.ds(pl.multiple_of(i * TCH, TCH), TCH)
+        x_t[:, tok] = x_ref[tok, :].T
+        block = (dht_ref[:, tok] * scale).astype(BF)
+        grad_t[:, tok] = block
+        grad[tok, :] = block.T
+        return carry
+
+    blocks = ff // FB
 
     def unit(u, carry):
-        tok = pl.ds(pl.multiple_of(lax.div(u, 2) * CH, CH), CH)
-        first = lax.rem(u, 2) * (ff // 2)
-        xs, grad_t = x_ref[tok, :], (dht_ref[:, tok] * scale).astype(BF)
-        x_t, grad = xs.T, grad_t.T
-        for f in range(0, ff // 2, FB):
-            at = pl.ds(pl.multiple_of(first + f, FB), FB)
-            act, slope = gelu_pair(dot(xs, w1_ref[:, at]))
-            q = (slope * dot_nt(grad, w2_ref[at, :])).astype(BF)
-            dw2t_ref[:, at] += dot(grad_t, act.astype(BF))
-            dw1_ref[:, at] += dot(x_t, q)
+        tok = pl.ds(pl.multiple_of(lax.div(u, blocks) * TCH, TCH), TCH)
+        at = pl.ds(pl.multiple_of(lax.rem(u, blocks) * FB, FB), FB)
+        act, slope = gelu_pair(dot(x_ref[tok, :], w1_ref[:, at]))
+        q = (slope * dot_nt(grad[tok, :], w2_ref[at, :])).astype(BF)
+        dw2t_ref[:, at] += dot(grad_t[:, tok], act.astype(BF))
+        dw1_ref[:, at] += dot(x_t[:, tok], q)
         return carry
 
-    pair_copy.wait()
-    work[...] = work[...] + r0[...]
-    step = [send(1, work.at[rows((1 - x) * p2, p2), :], r1.at[0], x_peer),
-            send(2, work.at[rows(p1 + (1 - y) * p2, p2), :], r1.at[1], y_peer)]
-    lax.fori_loop(0, 5, unit, 0)
-    for copy in step:
-        copy.wait()
-    for at, k in ((rows(x * p2, p2), 0), (rows(p1 + y * p2, p2), 1)):
-        work[at, :] = work[at, :] + r1[k]
-    step = [send(3, work.at[rows(x * p2 + (1 - y) * p3, p3), :], r2.at[0], y_peer),
-            send(4, work.at[rows(p1 + y * p2 + (1 - x) * p3, p3), :], r2.at[1], x_peer)]
-    lax.fori_loop(5, 2 * (x_ref.shape[0] // CH), unit, 0)
-    for copy in step:
-        copy.wait()
-    piece_a, piece_b = x * p2 + y * p3, p1 + y * p2 + x * p3
-    step = []
-    for k, piece, peer in ((0, piece_a, y_peer), (1, piece_b, x_peer)):
-        at = rows(mine + piece, p3)
-        sum_ref[at, :] = work[rows(piece, p3), :] + r2[k]
-        step.append(send(5 + k, sum_ref.at[at, :], sum_ref.at[at, :], peer))
-    for copy in step:
-        copy.wait()
-    at_a, at_b = rows(mine + x * p2, p2), rows(mine + p1 + y * p2, p2)
-    step = [send(7, sum_ref.at[at_a, :], sum_ref.at[at_a, :], x_peer), send(8, sum_ref.at[at_b, :], sum_ref.at[at_b, :], y_peer)]
-    last = [send(9, sum_ref.at[at_a, :], sum_ref.at[at_a, :], pair), send(10, sum_ref.at[at_b, :], sum_ref.at[at_b, :], pair)]
+    units = toks // TCH * blocks
+    wait(step[0])
+    step[0] = stage1(0)
+    wait(step[1])
+    step[1] = stage1(1)
+    lax.fori_loop(0, toks // TCH, turn, 0)
+    lax.fori_loop(0, units // 4, unit, 0)
+    wait(step[0])
+    step[0] = stage2(0)
+    lax.fori_loop(units // 4, units // 2, unit, 0)
+    wait(step[1])
+    step[1] = stage2(1)
+    lax.fori_loop(units // 2, units * 5 // 8, unit, 0)
+    wait(step[0])
+    step[0] = stage3(0)
+    lax.fori_loop(units * 5 // 8, units * 3 // 4, unit, 0)
+    wait(step[1])
+    step[1] = stage3(1)
+    lax.fori_loop(units * 3 // 4, units, unit, 0)
+    wait(step[0])
+    step[0], last0 = stage4(0)
+    wait(step[1])
+    step[1], last1 = stage4(1)
     stores = [pltpu.make_async_copy(dw1_ref, dw1_hbm, store_sem.at[0]), pltpu.make_async_copy(flip.at[0], dw2_hbm, store_sem.at[1])]
     stores[0].start()
     for f in range(0, ff, FB):
         flip[0, f : f + FB, :] = dw2t_ref[:, f : f + FB].T
     stores[1].start()
-    for copy in step:
-        copy.wait()
-    at_a, at_b = rows(mine + (1 - x) * p2, p2), rows(mine + p1 + (1 - y) * p2, p2)
-    last += [send(11, sum_ref.at[at_a, :], sum_ref.at[at_a, :], pair), send(12, sum_ref.at[at_b, :], sum_ref.at[at_b, :], pair)]
-    for copy in last:
-        copy.wait()
+    wait(step[0])
+    last0 += stage5(0)
+    wait(last0)
     stores += [pltpu.make_async_copy(sum_ref.at[rows(0, dim), :], dwi1_hbm, store_sem.at[2]), pltpu.make_async_copy(flip.at[1], dwi2_hbm, store_sem.at[3])]
     stores[2].start()
+    wait(step[1])
+    last1 += stage5(1)
+    wait(last1)
     for f in range(0, ff, FB):
         flip[1, f : f + FB, :] = sum_ref[dim:, f : f + FB].T
     stores[3].start()
-    for copy in stores:
-        copy.wait()
+    wait(stores)
 
 
 def exchange(n, src_ref, all_ref, send_sem, recv_sem):
@@ -493,7 +537,7 @@
             tower_back_kernel, "tower_back", 8 * cap * dim * ff // 4,
             [(starts, None), (wi_one, True), (wi_two, True), (attr, True), (g, False), (rows, False), (pre, False)],
             [(sds(rows_loc, dim), False), (sds(2 * dim, ff), True)],
-            [pltpu.VMEM((cap + CH, dim), BF), pltpu.VMEM((4, BLK, dim), F32), pltpu.SMEM((2,), jnp.int32), pltpu.SemaphoreType.DMA((4,))])
+            [pltpu.VMEM((cap + CH, dim), BF), pltpu.VMEM((8, BLK, dim), F32), pltpu.SMEM((2,), jnp.int32), pltpu.SemaphoreType.DMA((8,))])
 
         any_spec = pl.BlockSpec(memory_space=pl.ANY)
         dw_one, dw_two, dwi_one, dwi_two = pl.pallas_call(
@@ -502,10 +546,11 @@
             out_shape=[sds(dim, ff), sds(ff, dim), sds(dim, ff), sds(ff, dim)],
             scratch_shapes=[
                 pltpu.VMEM((dim, ff), F32), pltpu.VMEM((dim, ff), F32), pltpu.VMEM((2 * dim, ff), F32), pltpu.VMEM((2, ff, dim), F32),
-                pltpu.VMEM((toks, dim), BF), pltpu.VMEM((dim, toks), F32), pltpu.VMEM((dim, ff), BF), pltpu.VMEM((ff, dim), BF),
-                pltpu.VMEM((dim, ff), F32), pltpu.VMEM((dim, ff), F32),
-                pltpu.VMEM((2, dim // 4, ff), F32), pltpu.VMEM((2, dim // 8, ff), F32),
-                pltpu.SemaphoreType.DMA((5,)), pltpu.SemaphoreType.DMA((4,)), pltpu.SemaphoreType.DMA((13,)), pltpu.SemaphoreType.DMA((13,))],
+                pltpu.VMEM((toks, dim), BF), pltpu.VMEM((dim, toks), BF), pltpu.VMEM((dim, toks), F32), pltpu.VMEM((dim, toks), BF),
+                pltpu.VMEM((toks, dim), BF), pltpu.VMEM((dim, ff), BF), pltpu.VMEM((ff, dim), BF),
+                pltpu.VMEM((2, dim // 2, ff), F32), pltpu.VMEM((2, dim // 2, ff), F32),
+                pltpu.VMEM((2, 2, dim // 8, ff), F32), pltpu.VMEM((2, 2, dim // 16, ff), F32),
+                pltpu.SemaphoreType.DMA((6,)), pltpu.SemaphoreType.DMA((4,)), pltpu.SemaphoreType.DMA((26,)), pltpu.SemaphoreType.DMA((26,))],
             compiler_params=pltpu.CompilerParams(vmem_limit_bytes=VMEM_LIMIT, collective_id=2, has_side_effects=True),
             cost_estimate=cost(8 * toks * dim * ff), name="query_back",
         )(x_all, dht, w_one, w_two, dwi_part)

time: 362 us -> 346 us (0.956)
  Pallas kernels: 309 us -> 293 us
    pallas_call x3, Pallas kernels: 185 us -> 177 us  [call(): pl.pallas_call(kernel, in_specs=[spec(None)] + [spec(p) for _, p in ins],...]
    pallas_call x1, Pallas kernels: 88.3 us -> 80.6 us  [local_step(): pl.pallas_call(functools.partial(query_back_kernel, scale), in_specs=[any...]
where the time goes in v2:
time: 346 us
  Pallas kernels  293 us (85%)
  between operations  17 us (5%)
  local copies, waits for them, and re-layouts  15.6 us (5%)
  other arithmetic  14.5 us (4%)
  matrix products  4.61 us (1%)
    pallas_call x3, Pallas kernels, call(): pl.pallas_call(kernel, in_specs=[spec(None)] + [spec(p) for _, p in ins],...  177 us
    pallas_call x1, Pallas kernels, local_step(): pl.pallas_call(functools.partial(query_back_kernel, scale), in_specs=[any...  80.6 us
    pallas_call x1, Pallas kernels, local_step(): pl.pallas_call(gather_kernel, grid_spec=pltpu.PrefetchScalarGridSpec(num_...  21.8 us
    unnamed x22, local copies, waits for them, and re-layouts  15 us
    pallas_call x2, Pallas kernels, share(): pl.pallas_call(functools.partial(kernel, n), out_shape=out, in_specs=[vme...  14.1 us
    sort x1, other arithmetic, local_step(): key_s, offs_s = lax.sort((key, offs), num_keys=1, is_stable=False)  8.22 us
  transfers between devices with their start and end apart: 3, of which 0 were waited for; matrix products, arithmetic and copies ran while one was open for 4% of the time, Pallas kernels for 49%

profile of v2, /device:TPU:0, one launch (start us, length us, event | category | flops | bytes accessed | tf_op | source)
XLA Modules:
  0.0 345.8 jit_solution(3286976036433854719)
XLA Ops:
  7.2 0.0 copy-start.3
  7.2 0.0 copy-start.6
  7.2 0.0 copy-start.5
  7.2 0.0 all-gather.3.cloned.1.call-start
  7.2 4.6 %convolution_convert_fusion = bf16[256,512]{1,0:T(8,128)(2,1)} fusion(bf16[2048,512]{1,0:T(8,128)(2,1)} %w2_hbm.1, bf16[256,512]{1,0:T(8,128)(2,1)} %param.10, bf16[512,2048]{1,0:T(8,128)(2,1)} %w1_hbm.1), kind=kOutput, calls=%fused_computation.10 | convolution fusion | flops 1078591488 | bytes 4718592 | tf_op jit(solution)/shard_map/dot_general | solution.py:459
  11.9 0.0 copy-start.8
  11.9 0.0 all-gather.3.cloned.1.call-update
  11.9 0.0 all-gather.5.cloned.1.call-start
  11.9 0.7 all-gather.5.cloned.1.call-update
  12.6 0.0 all-reduce.4.cloned.1.call-start
  12.7 7.8 %shard_map.145 = s32[8,1,256]{2,1,0:T(1,128)} custom-call(s32[1,256]{1,0:T(1,128)} %bitcast.21), custom_call_target="tpu_custom_call" | custom-call | tf_op jit(solution)/shard_map/pallas_call | solution.py:426
  20.6 0.0 copy-done.6
  20.6 1.3 subtract_convert_fusion
  21.9 0.0 copy-done.3
  21.9 0.0 copy-done.5
  21.9 0.7 add_select_fusion
  22.6 8.2 %sort.15 = (s32[18432]{0:T(1024)S(1)}, f32[18432]{0:T(1024)S(1)}) sort(s32[18432]{0:T(1024)S(1)} %add_select_fusion, f32[18432]{0:T(1024)S(1)} %concatenate.20), dimensions={0}, to_apply=%region_1.2 | sort | flops 276480 | bytes 294912 | tf_op jit(solution)/shard_map/sort | solution.py:488
  30.8 0.1 slice_compare_fusion
  30.9 0.1 convert_select_fusion.1
  31.0 0.2 select_maximum_fusion
  31.3 0.9 convert_reduce_fusion.starts_ref
  32.2 0.0 copy-start.7
  32.2 0.6 slice.12
  33.4 0.0 copy-done.8
  33.4 0.1 broadcast_in_dim.36
  33.5 0.9 maximum_bitcast_fusion.attr_ref.attr_hbm
  34.4 0.0 copy-done.7
  34.4 21.8 %gather.1.rows_hbm = bf16[18432,512]{1,0:T(8,128)(2,1)} custom-call(s32[65]{0:T(128)} %copy-done.7, s32[1]{0:T(128)} %bitcast.3.nch_ref, bf16[32768,512]{1,0:T(8,128)(2,1)} %tbl_ref.1, f32[148,8,128]{2,1,0:T(8,128)} %maximum_bitcast_fusion.attr_ref.attr_hbm), custom_call_target="tpu_custom_call" | custom-call | flops 8589934592 | bytes 67108864 | tf_op jit(solution)/shard_map/gather/pallas_call | solution.py:502
  56.2 0.0 all-gather.3.cloned.1.call-done.h_ref
  56.2 60.0 %fwd.1 = (bf16[18432,512]{1,0:T(8,128)(2,1)}, f32[18432,2048]{1,0:T(8,128)}, f32[18432,2048]{1,0:T(8,128)}, f32[2,2048]{1,0:T(2,128)}) custom-call(s32[1]{0:T(128)} %bitcast.3.nch_ref, f32[1,2048]{1,0:T(1,128)} %bitcast.19, bf16[2048,512]{1,0:T(8,128)(2,1)} %all-gather.3.cloned.1.call-done.h_ref, bf16[512,2048]{1,0:T(8,128)(2,1)} %w1_ref.3, ...), custom_call_target="tpu_custom_call" | custom-call | flops 28991029248 | bytes 67108864 | tf_op jit(solution)/shard_map/fwd/pallas_call | solution.py:514
  116.2 0.0 all-gather.5.cloned.1.call-done.x_hbm
  116.2 6.3 %shard_map.146.lse_ref = f32[1,2048]{1,0:T(1,128)} custom-call(f32[2,2048]{1,0:T(2,128)} %get-tuple-element.25.src_ref), custom_call_target="tpu_custom_call" | custom-call | tf_op jit(solution)/shard_map/pallas_call | solution.py:426
  122.5 35.7 %logit_back.1 = (bf16[18432,512]{1,0:T(8,128)(2,1)}, f32[520,2048]{1,0:T(8,128)}) custom-call(s32[1]{0:T(128)} %bitcast.3.nch_ref, f32[1,2048]{1,0:T(1,128)} %bitcast.20, f32[1,2048]{1,0:T(1,128)} %shard_map.146.lse_ref, bf16[2048,512]{1,0:T(8,128)(2,1)} %all-gather.3.cloned.1.call-done.h_ref, f32[18432,2048]{1,0:T(8,128)} %get-tuple-element.26.z_hbm, ...), custom_call_target="tpu_custom_call" | custom-call | flops 19327352832 | bytes 67108864 | tf_op jit(solution)/shard_map/logit_back/pallas_call | solution.py:514
  158.2 0.0 all-reduce.4.cloned.1.call-update
  158.2 0.7 copy-done.4
  158.9 0.6 reduce_sum.28
  159.5 80.9 %tower_back.1 = (f32[32768,512]{1,0:T(8,128)}, f32[1024,2048]{1,0:T(8,128)}) custom-call(s32[1]{0:T(128)} %bitcast.3.nch_ref, s32[65]{0:T(128)} %copy-done.7, bf16[512,2048]{1,0:T(8,128)(2,1)} %w1_ref.3, bf16[2048,512]{1,0:T(8,128)(2,1)} %w2_ref.3, f32[148,8,128]{2,1,0:T(8,128)} %maximum_bitcast_fusion.attr_ref.attr_hbm, ...), custom_call_target="tpu_custom_call" | custom-call | flops 38654705664 | bytes 67108864 | tf_op jit(solution)/shard_map/tower_back/pallas_call | solution.py:514
  240.4 0.0 all-reduce.4.cloned.1.call-done.dht_hbm
  240.4 80.6 %query_back.1 = (f32[512,2048]{1,0:T(8,128)}, f32[2048,512]{1,0:T(8,128)}, f32[512,2048]{1,0:T(8,128)}, f32[2048,512]{1,0:T(8,128)}) custom-call(bf16[2048,512]{1,0:T(8,128)(2,1)} %all-gather.5.cloned.1.call-done.x_hbm, f32[520,2048]{1,0:T(8,128)} %all-reduce.4.cloned.1.call-done.dht_hbm, bf16[512,2048]{1,0:T(8,128)(2,1)} %w1_hbm.1, ...), custom_call_target="tpu_custom_call" | custom-call | flops 17179869184 | bytes 67108864 | tf_op jit(solution)/shard_map/query_back/pallas_call | solution.py:543
  321.1 1.5 slice_reduce_fusion
  323.8 0.0 copy-start.2
  323.8 4.8 %copy.21 = f32[512,2048]{1,0:T(8,128)} copy(f32[512,2048]{1,0:T(8,128)} %get-tuple-element.49) | data formatting | bytes 8388608
  328.7 0.0 copy-done.2
  328.7 2.1 copy.22
  330.8 1.6 copy-done.1
  332.4 2.1 copy.23
  334.5 1.6 copy-done
  336.1 2.0 copy.24
  (5 shorter events, 0.0 us)
Async XLA Ops:
  7.2 14.7 %copy-start.3 = (s32[18432]{0:T(1024)S(1)}, s32[18432]{0:T(1024)}, u32[]{:S(2)}) copy-start(s32[18432]{0:T(1024)} %constant.24.clone.1) | copy-start | bytes 221188
  7.2 13.4 %copy-start.6 = (f32[16384]{0:T(1024)S(1)}, f32[16384]{0:T(1024)}, u32[]{:S(2)}) copy-start(f32[16384]{0:T(1024)} %param.17) | copy-start | bytes 196612
  7.2 14.7 %copy-start.5 = (s32[16384]{0:T(1024)S(1)}, s32[16384]{0:T(1024)}, u32[]{:S(2)}) copy-start(s32[16384]{0:T(1024)} %param.16) | copy-start | bytes 196612
  7.2 49.0 %all-gather.3.cloned.1.call-start = ((), (), s32[]{:S(2)}) async-start(), calls=%async_computation | async-start | bytes 2359296 | tf_op jit(solution)/shard_map/all_gather | solution.py:477
  11.9 21.6 %copy-start.8 = (f32[8]{0:T(128)S(1)}, f32[8]{0:T(128)}, u32[]{:S(2)}) copy-start(f32[8]{0:T(128)} %constant.56.clone) | copy-start | bytes 100
  11.9 104.3 %all-gather.5.cloned.1.call-start = ((), (), s32[]{:S(2)}) async-start(), calls=%async_computation.1 | async-start | bytes 2359296 | tf_op jit(solution)/shard_map/all_gather | solution.py:478
  12.6 227.8 %all-reduce.4.cloned.1.call-start = ((), (), s32[]{:S(2)}) async-start(), calls=%async_computation.2 | async-start | bytes 8519680 | tf_op jit(solution)/shard_map/psum | solution.py:535
  32.2 2.2 copy-start.7
  158.2 0.7 copy-start.4
  323.8 4.9 %copy-start.2 = (f32[2048,512]{1,0:T(8,128)S(1)}, f32[2048,512]{1,0:T(8,128)}, u32[]{:S(2)}) copy-start(f32[2048,512]{1,0:T(8,128)} %get-tuple-element.50) | copy-start | bytes 12582916
  328.7 3.7 %copy-start.1 = (f32[512,2048]{1,0:T(8,128)S(1)}, f32[512,2048]{1,0:T(8,128)}, u32[]{:S(2)}) copy-start(f32[512,2048]{1,0:T(8,128)} %get-tuple-element.51) | copy-start | bytes 12582916
  332.4 3.7 %copy-start = (f32[2048,512]{1,0:T(8,128)S(1)}, f32[2048,512]{1,0:T(8,128)}, u32[]{:S(2)}) copy-start(f32[2048,512]{1,0:T(8,128)} %get-tuple-element.52) | copy-start | bytes 12582916
Sparse Core Ops, SparseCore 0:
  12.0 24.8 all-gather.2
  38.7 21.9 all-gather.4
  158.4 68.8 all-reduce.3

commit v3 on v2

--- a/solution.py
+++ b/solution.py
@@ -16,6 +16,7 @@
 TCH = 512
 SUB = 8
 PAIR = 2
+GROUP = 4
 WIN = 128
 FB = 256
 TB = 256
@@ -94,7 +95,7 @@
         return dot(jnp.concatenate(pick, axis=1), tbl_ref[pl.ds(pl.multiple_of(part * BLK, BLK), BLK), :]).astype(BF)
 
     def some_blocks(i, carry):
-        parts = [i * PAIR + k for k in range(PAIR)]
+        parts = [i * GROUP + k for k in range(GROUP)]
         blks = [step * SUB + part for part in parts]
         firsts = [(starts_ref[blk] >> 4) << 4 for blk in blks]
         gots = [picked(blk, part, pl.multiple_of(first, 16)) for blk, part, first in zip(blks, parts, firsts)]
@@ -111,7 +112,7 @@
             lax.fori_loop(1, (starts_ref[blk + 1] - first + (WIN - 1)) >> 7, more, 0)
         return carry
 
-    lax.fori_loop(0, SUB // PAIR, some_blocks, 0)
+    lax.fori_loop(0, SUB // GROUP, some_blocks, 0)
 
     @pl.when(step == pl.num_programs(0) - 1)
     def _():
@@ -143,11 +144,10 @@
         u_ref[...] = vec
         loc = column(attr_ref, 0, 0, CH // WIN)
         off = column(attr_ref, 1, 0, CH // WIN)
-        is_targ = column(attr_ref, 2, 0, CH // WIN) > 0.5
         for t in range(0, toks, TB):
             raw = dot_nt(vec, h_ref[t : t + TB, :]) * scale
             same = loc == tid_ref[:, t : t + TB]
-            z = jnp.where(same, jnp.where(is_targ, raw, HIT_VALUE), raw - off)
+            z = raw - jnp.where(same, 0.0, off)
             z_ref[:, t : t + TB] = z
             z3 = z.reshape(CH // 8, 8, TB)
             old = m8[:, t : t + TB]
@@ -162,25 +162,22 @@
     stat_ref[1:2, :] = jnp.sum(s8[...] * jnp.exp(m8[...] - top), axis=0, keepdims=True)
 
 
-def logit_back_kernel(scale, nch_ref, tid_ref, lse_ref, h_ref, z_hbm, u_hbm, attr_hbm, g_hbm, dht_ref):
+def logit_back_kernel(scale, nch_ref, tid_ref, stat_ref, h_ref, z_hbm, u_hbm, attr_hbm, g_hbm, dht_ref):
     dht_ref[...] = jnp.zeros_like(dht_ref)
     dim, toks = u_hbm.shape[1], h_ref.shape[0]
 
     def body(z_ref, u_ref, attr_ref, g_ref):
         vec_t = u_ref[...].T
         loc = column(attr_ref, 0, 0, CH // WIN)
-        is_targ = column(attr_ref, 2, 0, CH // WIN)
-        shift = is_targ * (-1.0 / toks)
         grad = None
-        log_toks = math.log(toks)
         for t in range(0, toks, TB):
             z = z_ref[:, t : t + TB]
             same = loc == tid_ref[:, t : t + TB]
-            dz = (jnp.exp(z - (lse_ref[:, t : t + TB] + log_toks)) + jnp.where(same, shift, 0.0)).astype(BF)
+            dz = (jnp.exp(z - stat_ref[1:2, t : t + TB]) + jnp.where(same, stat_ref[2:3, t : t + TB], 0.0)).astype(BF)
             part = dot(dz, h_ref[t : t + TB, :])
             grad = part if grad is None else grad + part
             dht_ref[:dim, t : t + TB] += dot(vec_t, dz)
-            zt = jnp.where(same, z * is_targ, 0.0)
+            zt = jnp.where(same, z, 0.0)
             dht_ref[dim:, t : t + TB] += jnp.sum(zt.reshape(CH // 8, 8, TB), axis=0)
         g_ref[...] = (grad * scale).astype(BF)
 
@@ -402,32 +399,50 @@
             device_id=(lax.rem(me + k, n),), device_id_type=MESH))
         copies[-1].start()
     all_ref[me] = src_ref[...]
+    return copies
+
+
+def query_kernel(n, targ_ref, x_hbm, w1_hbm, w2_hbm, all_ref, out_ref, x_ref, w1_ref, w2_ref, load_sem, send_sem, recv_sem):
+    loads = [(x_hbm, x_ref), (w1_hbm, w1_ref), (w2_hbm, w2_ref)]
+    loads = [pltpu.make_async_copy(src, dst, load_sem.at[i]) for i, (src, dst) in enumerate(loads)]
+    for copy in loads:
+        copy.start()
+    copies = exchange(n, targ_ref, all_ref, send_sem, recv_sem)
+    for copy in loads:
+        copy.wait()
+    out = None
+    for f in range(0, w1_ref.shape[1], FB):
+        part = dot(gelu(dot(x_ref[...], w1_ref[:, f : f + FB])).astype(BF), w2_ref[f : f + FB, :])
+        out = part if out is None else out + part
+    out_ref[...] = out.astype(BF)
     for copy in copies:
         copy.wait()
 
 
-def targets_kernel(n, src_ref, out_ref, send_sem, recv_sem):
-    exchange(n, src_ref, out_ref, send_sem, recv_sem)
-
-
-def stats_kernel(n, src_ref, lse_ref, stats, send_sem, recv_sem):
-    exchange(n, src_ref, stats, send_sem, recv_sem)
-    top = stats[0, 0:1, :]
-    for i in range(1, n):
+def stats_kernel(n, stat_ref, hit_ref, out_ref, stats, send_sem, recv_sem):
+    for copy in exchange(n, stat_ref, stats, send_sem, recv_sem):
+        copy.wait()
+    toks = stat_ref.shape[1]
+    hit = hit_ref[...] > 0.5
+    top = jnp.where(hit, HIT_VALUE, -EXCLUDED)
+    for i in range(n):
         top = jnp.maximum(top, stats[i, 0:1, :])
-    total = jnp.zeros_like(top)
+    total = jnp.where(hit, jnp.exp(HIT_VALUE - top), 0.0)
     for i in range(n):
         total += stats[i, 1:2, :] * jnp.exp(stats[i, 0:1, :] - top)
-    lse_ref[...] = top + jnp.log(total)
-
-
-def share(kernel, ident, n, src, out, scratch=()):
-    vmem = pl.BlockSpec(memory_space=pltpu.VMEM)
+    lse = top + jnp.log(total)
+    out_ref[0:1, :] = lse
+    out_ref[1:2, :] = lse + math.log(toks)
+    out_ref[2:3, :] = jnp.where(hit, jnp.exp(HIT_VALUE - (lse + math.log(toks))), 0.0) - 1.0 / toks
+
+
+def share(kernel, ident, n, ins, out, scratch=()):
+    spec = lambda place: pl.BlockSpec(memory_space=pltpu.VMEM if place else pl.ANY)
     return pl.pallas_call(
-        functools.partial(kernel, n), out_shape=out, in_specs=[vmem], out_specs=vmem,
+        functools.partial(kernel, n), out_shape=out, in_specs=[spec(p) for _, p in ins], out_specs=[spec(True) for _ in out],
         scratch_shapes=[*scratch, pltpu.SemaphoreType.DMA((n - 1,)), pltpu.SemaphoreType.DMA((n - 1,))],
-        compiler_params=pltpu.CompilerParams(collective_id=ident, has_side_effects=True),
-    )(src)
+        compiler_params=pltpu.CompilerParams(collective_id=ident, has_side_effects=True, vmem_limit_bytes=VMEM_LIMIT),
+    )(*[a for a, _ in ins])
 
 
 def params(**kw):
@@ -451,12 +466,6 @@
 
 def sds(*shape, dtype=F32):
     return jax.ShapeDtypeStruct(shape, dtype)
-
-
-def query_fwd(x, w_in, w_out):
-    pre = jnp.dot(x, w_in, preferred_element_type=F32)
-    hidden = jax.nn.gelu(pre).astype(BF)
-    return jnp.dot(hidden, w_out, preferred_element_type=F32).astype(BF)
 
 
 def solution(mesh):
@@ -473,12 +482,17 @@
         scale = SCORE_GAIN / math.sqrt(dim)
         base = lax.axis_index("dp") * rows_loc
 
-        query_loc = query_fwd(tokens, w_one, w_two)
+        hit = jnp.any(targ_loc[:, None] == cand_ids[None, :], axis=1)
+        coded, query_loc = share(
+            query_kernel, 0, num_dev, [((2 * targ_loc + hit)[None, :], True), (tokens, False), (w_one, False), (w_two, False)],
+            [sds(num_dev, 1, targ_loc.shape[0], dtype=jnp.int32), sds(*tokens.shape, dtype=BF)],
+            [pltpu.VMEM(tokens.shape, BF), pltpu.VMEM(w_one.shape, BF), pltpu.VMEM(w_two.shape, BF), pltpu.SemaphoreType.DMA((3,))])
+        coded = coded.reshape(toks)
+        targ_all, hit_all = coded >> 1, coded & 1
         query = lax.all_gather(query_loc, "dp", axis=0, tiled=True)
         x_all = lax.all_gather(tokens, "dp", axis=0, tiled=True)
-        targ_all = share(targets_kernel, 0, num_dev, targ_loc[None, :], sds(num_dev, 1, targ_loc.shape[0], dtype=jnp.int32)).reshape(toks)
-
-        ids = jnp.concatenate([cand_ids, targ_all]) - base
+
+        ids = jnp.concatenate([cand_ids, jnp.where(hit_all == 1, -1, targ_all)]) - base
         kind = jnp.concatenate([jnp.zeros((cands,), jnp.int32), jnp.ones((toks,), jnp.int32)])
         key = jnp.where((ids >= 0) & (ids < rows_loc), 2 * ids + kind, 2 * rows_loc)
         offs = jnp.concatenate([log_q, jnp.full((toks,), EXCLUDED, F32)])
@@ -491,9 +505,8 @@
         attr = jnp.stack([
             jnp.where(used, (key_s >> 1).astype(F32), NO_ROW),
             jnp.where(used, offs_s, EXCLUDED),
-            jnp.where(used, (key_s & 1).astype(F32), 0.0),
         ])
-        attr = jnp.pad(attr, ((0, 5), (0, 0)))
+        attr = jnp.pad(attr, ((0, 6), (0, 0)))
         pad = jnp.broadcast_to(jnp.array([NO_ROW, EXCLUDED, 0, 0, 0, 0, 0, 0], F32)[:, None], (8, CH))
         attr = jnp.concatenate([attr, pad], axis=1).reshape(8, -1, WIN).transpose(1, 0, 2)
         tid = (targ_all - base).astype(F32)[None, :]
@@ -525,11 +538,13 @@
             [pltpu.VMEM((8, toks), F32), pltpu.VMEM((8, toks), F32)])
 
         stat, x_all = lax.optimization_barrier((stat, x_all))
-        lse = share(stats_kernel, 1, num_dev, stat, sds(1, toks), [pltpu.VMEM((num_dev, 2, toks), F32)])
+        (stat,) = share(
+            stats_kernel, 1, num_dev, [(stat, True), (hit_all.astype(F32)[None, :], True)], [sds(3, toks)],
+            [pltpu.VMEM((num_dev, 2, toks), F32)])
 
         g, dht_part = call(
             functools.partial(logit_back_kernel, scale), "logit_back", 4 * cap * dim * toks // 4,
-            [(tid, True), (lse, True), (query, True), (z, False), (vec, False), (attr, False)],
+            [(tid, True), (stat, True), (query, True), (z, False), (vec, False), (attr, False)],
             [(bf_list, False), (sds(dim + 8, toks), True)])
 
         dht = lax.psum(dht_part, "dp")
@@ -539,6 +554,8 @@
             [(sds(rows_loc, dim), False), (sds(2 * dim, ff), True)],
             [pltpu.VMEM((cap + CH, dim), BF), pltpu.VMEM((8, BLK, dim), F32), pltpu.SMEM((2,), jnp.int32), pltpu.SemaphoreType.DMA((8,))])
 
+        loss = (jnp.sum(stat[0]) - jnp.sum(dht[dim:])) / toks
+        dht, loss = lax.optimization_barrier((dht, loss))
         any_spec = pl.BlockSpec(memory_space=pl.ANY)
         dw_one, dw_two, dwi_one, dwi_two = pl.pallas_call(
             functools.partial(query_back_kernel, scale),
@@ -555,7 +572,6 @@
             cost_estimate=cost(8 * toks * dim * ff), name="query_back",
         )(x_all, dht, w_one, w_two, dwi_part)
 
-        loss = (jnp.sum(lse) - jnp.sum(dht[dim:])) / toks
         return loss, d_table, dw_one, dw_two, dwi_one, dwi_two
 
     return jax.shard_map(local_step, mesh=mesh, in_specs=(P("dp", None), P(), P(), P(), P(), P("dp", None), P(), P(), P("dp")), out_specs=(P(), P("dp", None), P(), P(), P(), P()), check_vma=False)

time: 346 us -> 329 us (0.951)
  Pallas kernels: 293 us -> 277 us
  matrix products: 4.61 us -> 0 us
  other arithmetic: 14.5 us -> 18.9 us
    pallas_call x3, Pallas kernels: 177 us -> 160 us  [call(): pl.pallas_call(kernel, in_specs=[spec(None)] + [spec(p) for _, p in ins],...]
    dot_general x1 -> x0, matrix products: 4.61 us -> none  [query_fwd(): return jnp.dot(hidden, w_out, preferred_element_type=F32).astype(BF)]
    unnamed x22 -> x20, local copies, waits for them, and re-layouts: 15 us -> 14.3 us
  transfers between devices with their start and end apart: 3 -> 3, of which waited for: 0 -> 0; matrix products, arithmetic and copies ran while one was open for 4% -> 4% of each run, Pallas kernels for 49% -> 45%
where the time goes in v3:
time: 329 us
  Pallas kernels  277 us (84%)
  other arithmetic  18.9 us (6%)
  between operations  17 us (5%)
  local copies, waits for them, and re-layouts  15 us (5%)
    pallas_call x3, Pallas kernels, call(): pl.pallas_call(kernel, in_specs=[spec(None)] + [spec(p) for _, p in ins],...  160 us
    pallas_call x1, Pallas kernels, local_step(): pl.pallas_call(functools.partial(query_back_kernel, scale), in_specs=[any...  81.5 us
    pallas_call x1, Pallas kernels, local_step(): pl.pallas_call(gather_kernel, grid_spec=pltpu.PrefetchScalarGridSpec(num_...  20.1 us
    pallas_call x2, Pallas kernels, share(): pl.pallas_call(functools.partial(kernel, n), out_shape=out, in_specs=[spe...  14.5 us
    unnamed x20, local copies, waits for them, and re-layouts  14.3 us
    sort x1, other arithmetic, local_step(): key_s, offs_s = lax.sort((key, offs), num_keys=1, is_stable=False)  8.22 us
  transfers between devices with their start and end apart: 3, of which 0 were waited for; matrix products, arithmetic and copies ran while one was open for 4% of the time, Pallas kernels for 45%

profile of v3, /device:TPU:0, one launch (start us, length us, event | category | flops | bytes accessed | tf_op | source)
XLA Modules:
  0.0 328.5 jit_solution(10390313211893708361)
XLA Ops:
  7.2 0.0 copy-start.4
  7.2 0.0 copy-start.7
  7.2 0.0 copy-start.3
  7.2 0.0 copy-start.5
  7.2 0.0 all-gather.3.cloned.1.call-start
  7.3 3.2 compare_reduce_fusion
  10.4 1.2 convert_add_fusion
  11.7 8.2 %shard_map.145 = (s32[8,1,256]{2,1,0:T(1,128)}, bf16[256,512]{1,0:T(8,128)(2,1)}) custom-call(s32[1,256]{1,0:T(1,128)} %bitcast.18, bf16[256,512]{1,0:T(8,128)(2,1)} %x_hbm.1, bf16[512,2048]{1,0:T(8,128)(2,1)} %w1_hbm.3, bf16[2048,512]{1,0:T(8,128)(2,1)} %w2_hbm.3), custom_call_target="tpu_custom_call" | custom-call | tf_op jit(solution)/shard_map/pallas_call | solution.py:441
  19.9 0.0 all-gather.3.cloned.1.call-update
  19.9 0.0 all-gather.5.cloned.1.call-start
  20.0 0.7 all-gather.5.cloned.1.call-update
  20.7 0.2 all-reduce.4.cloned.1.call-start
  20.9 1.3 and_convert_fusion
  22.2 0.0 copy-done.4
  22.2 0.0 copy-done.3
  22.3 0.0 copy-done.5
  22.3 8.2 %sort.15 = (s32[18432]{0:T(1024)S(1)}, f32[18432]{0:T(1024)S(1)}) sort(s32[18432]{0:T(1024)S(1)} %add_select_fusion, f32[18432]{0:T(1024)S(1)} %concatenate.17), dimensions={0}, to_apply=%region_2.3 | sort | flops 276480 | bytes 294912 | tf_op jit(solution)/shard_map/sort | solution.py:502
  30.5 0.1 slice_compare_fusion
  30.6 0.1 convert_select_fusion
  30.7 0.2 select_maximum_fusion
  30.9 0.9 convert_reduce_fusion.starts_ref
  31.8 0.0 copy-start.6
  31.8 0.6 slice.15
  33.0 0.0 copy-done.7
  33.0 0.1 broadcast_in_dim.40
  33.1 0.9 maximum_bitcast_fusion.attr_ref.attr_hbm
  34.0 0.0 copy-done.6
  34.0 20.1 %gather.1.rows_hbm = bf16[18432,512]{1,0:T(8,128)(2,1)} custom-call(s32[65]{0:T(128)} %copy-done.6, s32[1]{0:T(128)} %bitcast.3.nch_ref, bf16[32768,512]{1,0:T(8,128)(2,1)} %tbl_ref.1, f32[148,8,128]{2,1,0:T(8,128)} %maximum_bitcast_fusion.attr_ref.attr_hbm), custom_call_target="tpu_custom_call" | custom-call | flops 8589934592 | bytes 67108864 | tf_op jit(solution)/shard_map/gather/pallas_call | solution.py:515
  54.1 0.0 all-gather.3.cloned.1.call-done.h_ref
  54.1 52.5 %fwd.1 = (bf16[18432,512]{1,0:T(8,128)(2,1)}, f32[18432,2048]{1,0:T(8,128)}, f32[18432,2048]{1,0:T(8,128)}, f32[2,2048]{1,0:T(2,128)}) custom-call(s32[1]{0:T(128)} %bitcast.3.nch_ref, f32[1,2048]{1,0:T(1,128)} %bitcast.14, bf16[2048,512]{1,0:T(8,128)(2,1)} %all-gather.3.cloned.1.call-done.h_ref, bf16[512,2048]{1,0:T(8,128)(2,1)} %w1_ref.3, ...), custom_call_target="tpu_custom_call" | custom-call | flops 28991029248 | bytes 67108864 | tf_op jit(solution)/shard_map/fwd/pallas_call | solution.py:527
  106.6 6.3 %shard_map.146.stat_ref = f32[3,2048]{1,0:T(4,128)} custom-call(f32[2,2048]{1,0:T(2,128)} %get-tuple-element.31.stat_ref, f32[1,2048]{1,0:T(1,128)} %bitcast.17), custom_call_target="tpu_custom_call" | custom-call | tf_op jit(solution)/shard_map/pallas_call | solution.py:441
  112.9 1.4 slice_reduce_fusion.1
  114.3 32.2 %logit_back.1 = (bf16[18432,512]{1,0:T(8,128)(2,1)}, f32[520,2048]{1,0:T(8,128)}) custom-call(s32[1]{0:T(128)} %bitcast.3.nch_ref, f32[1,2048]{1,0:T(1,128)} %bitcast.15, f32[3,2048]{1,0:T(4,128)} %shard_map.146.stat_ref, bf16[2048,512]{1,0:T(8,128)(2,1)} %all-gather.3.cloned.1.call-done.h_ref, f32[18432,2048]{1,0:T(8,128)} %get-tuple-element.32.z_hbm, ...), custom_call_target="tpu_custom_call" | custom-call | flops 19327352832 | bytes 67108864 | tf_op jit(solution)/shard_map/logit_back/pallas_call | solution.py:527
  146.5 0.0 all-reduce.4.cloned.1.call-update
  146.5 75.7 %tower_back.1 = (f32[32768,512]{1,0:T(8,128)}, f32[1024,2048]{1,0:T(8,128)}) custom-call(s32[1]{0:T(128)} %bitcast.3.nch_ref, s32[65]{0:T(128)} %copy-done.6, bf16[512,2048]{1,0:T(8,128)(2,1)} %w1_ref.3, bf16[2048,512]{1,0:T(8,128)(2,1)} %w2_ref.3, f32[148,8,128]{2,1,0:T(8,128)} %maximum_bitcast_fusion.attr_ref.attr_hbm, ...), custom_call_target="tpu_custom_call" | custom-call | flops 38654705664 | bytes 67108864 | tf_op jit(solution)/shard_map/tower_back/pallas_call | solution.py:527
  222.2 0.0 all-reduce.4.cloned.1.call-done.dht_hbm
  222.3 1.5 slice_reduce_fusion
  225.0 81.5 %query_back.1 = (f32[512,2048]{1,0:T(8,128)}, f32[2048,512]{1,0:T(8,128)}, f32[512,2048]{1,0:T(8,128)}, f32[2048,512]{1,0:T(8,128)}) custom-call(bf16[2048,512]{1,0:T(8,128)(2,1)} %all-gather.5.cloned.1.call-done.x_hbm, f32[520,2048]{1,0:T(8,128)} %all-reduce.4.cloned.1.call-done.dht_hbm, bf16[512,2048]{1,0:T(8,128)(2,1)} %w1_hbm.3, ...), custom_call_target="tpu_custom_call" | custom-call | flops 17179869184 | bytes 67108864 | tf_op jit(solution)/shard_map/query_back/pallas_call | solution.py:560
  306.6 0.0 copy-start.2
  306.6 4.8 %copy.21 = f32[512,2048]{1,0:T(8,128)} copy(f32[512,2048]{1,0:T(8,128)} %get-tuple-element.59) | data formatting | bytes 8388608
  311.4 0.0 copy-done.2
  311.4 0.0 copy-start.1
  311.4 2.1 copy.22
  313.6 1.6 copy-done.1
  315.1 0.0 copy-start
  315.1 2.1 copy.23
  317.3 1.6 copy-done
  318.8 2.0 copy.24
  (4 shorter events, 0.0 us)
Async XLA Ops:
  7.2 15.1 %copy-start.4 = (s32[18432]{0:T(1024)S(1)}, s32[18432]{0:T(1024)}, u32[]{:S(2)}) copy-start(s32[18432]{0:T(1024)} %constant.25.clone.1) | copy-start | bytes 221188
  7.2 25.8 %copy-start.7 = (f32[8]{0:T(128)S(1)}, f32[8]{0:T(128)}, u32[]{:S(2)}) copy-start(f32[8]{0:T(128)} %constant.54.clone) | copy-start | bytes 100
  7.2 15.0 %copy-start.3 = (s32[16384]{0:T(1024)S(1)}, s32[16384]{0:T(1024)}, u32[]{:S(2)}) copy-start(s32[16384]{0:T(1024)} %param.16) | copy-start | bytes 196612
  7.2 15.1 %copy-start.5 = (f32[16384]{0:T(1024)S(1)}, f32[16384]{0:T(1024)}, u32[]{:S(2)}) copy-start(f32[16384]{0:T(1024)} %param.17) | copy-start | bytes 196612
  7.2 46.9 %all-gather.3.cloned.1.call-start = ((), (), s32[]{:S(2)}) async-start(), calls=%async_computation | async-start | bytes 2359296 | tf_op jit(solution)/shard_map/all_gather | solution.py:492
  19.9 86.7 %all-gather.5.cloned.1.call-start = ((), (), s32[]{:S(2)}) async-start(), calls=%async_computation.1 | async-start | bytes 2359296 | tf_op jit(solution)/shard_map/all_gather | solution.py:493
  20.7 201.6 %all-reduce.4.cloned.1.call-start = ((), (), s32[]{:S(2)}) async-start(), calls=%async_computation.2 | async-start | bytes 8519680 | tf_op jit(solution)/shard_map/psum | solution.py:550
  31.8 2.2 copy-start.6
  306.6 4.9 %copy-start.2 = (f32[2048,512]{1,0:T(8,128)S(1)}, f32[2048,512]{1,0:T(8,128)}, u32[]{:S(2)}) copy-start(f32[2048,512]{1,0:T(8,128)} %get-tuple-element.60) | copy-start | bytes 12582916
  311.4 3.7 %copy-start.1 = (f32[512,2048]{1,0:T(8,128)S(1)}, f32[512,2048]{1,0:T(8,128)}, u32[]{:S(2)}) copy-start(f32[512,2048]{1,0:T(8,128)} %get-tuple-element.61) | copy-start | bytes 12582916
  315.1 3.7 %copy-start = (f32[2048,512]{1,0:T(8,128)S(1)}, f32[2048,512]{1,0:T(8,128)}, u32[]{:S(2)}) copy-start(f32[2048,512]{1,0:T(8,128)} %get-tuple-element.62) | copy-start | bytes 12582916
Sparse Core Ops, SparseCore 0:
  20.0 22.8 all-gather.2
  44.7 21.9 all-gather.4
  146.7 68.8 all-reduce.3

commit v4 on v3

--- a/solution.py
+++ b/solution.py
@@ -19,7 +19,8 @@
 GROUP = 4
 WIN = 128
 FB = 256
-TB = 256
+FWD_FB = 512
+TB = 512
 GELU_C = math.sqrt(2.0 / math.pi)
 BF, F32 = jnp.bfloat16, jnp.float32
 MESH = pl.DeviceIdType.MESH
@@ -134,11 +135,11 @@
     def body(rows_ref, attr_ref, u_ref, pre_ref, z_ref):
         rows = rows_ref[...]
         out = None
-        for f in range(0, ff, FB):
-            pre = dot(rows, w1_ref[:, f : f + FB])
-            pre_ref[:, f : f + FB] = pre
+        for f in range(0, ff, FWD_FB):
+            pre = dot(rows, w1_ref[:, f : f + FWD_FB])
+            pre_ref[:, f : f + FWD_FB] = pre
             act = gelu(pre).astype(BF)
-            part = dot(act, w2_ref[f : f + FB, :])
+            part = dot(act, w2_ref[f : f + FWD_FB, :])
             out = part if out is None else out + part
         vec = out.astype(BF)
         u_ref[...] = vec
@@ -251,8 +252,8 @@
         write(jnp.int32(blk)).wait()
 
 
-def query_back_kernel(scale, x_hbm, dht_hbm, w1_hbm, w2_hbm, part_hbm, dw1_hbm, dw2_hbm, dwi1_hbm, dwi2_hbm,
-                      dw1_ref, dw2t_ref, sum_ref, flip, x_ref, x_t, dht_ref, grad_t, grad, w1_ref, w2_ref, work, r0, r1, r2,
+def query_back_kernel(scale, stat_ref, x_hbm, dht_hbm, w1_hbm, w2_hbm, part_hbm, dw1_hbm, dw2_hbm, dwi1_hbm, dwi2_hbm, loss_ref,
+                      zt_ref, dw1_ref, dw2t_ref, sum_ref, flip, x_ref, x_t, dht_ref, grad_t, grad, w1_ref, w2_ref, work, r0, r1, r2,
                       load_sem, store_sem, send_sem, recv_sem):
     me = lax.axis_index("dp")
     core, x, y = lax.rem(me, 2), lax.rem(lax.div(me, 2), 2), lax.div(me, 4)
@@ -317,13 +318,16 @@
 
     step = [stage0(0), stage0(1)]
     loads = [(part_hbm.at[rows(mine(j), half), :], work.at[j]) for j in range(2)]
-    loads += [(x_hbm, x_ref), (dht_hbm.at[rows(0, dim), :], dht_ref), (w1_hbm, w1_ref), (w2_hbm, w2_ref)]
+    loads += [(x_hbm, x_ref), (dht_hbm.at[rows(0, dim), :], dht_ref), (w1_hbm, w1_ref), (w2_hbm, w2_ref), (dht_hbm.at[rows(dim, 8), :], zt_ref)]
     loads = [pltpu.make_async_copy(src, dst, load_sem.at[i]) for i, (src, dst) in enumerate(loads)]
     for copy in loads:
         copy.start()
     dw1_ref[...] = jnp.zeros_like(dw1_ref)
     dw2t_ref[...] = jnp.zeros_like(dw2t_ref)
     wait(loads)
+
+    total = jnp.sum(stat_ref[0:1, :], axis=1, keepdims=True) - jnp.sum(jnp.sum(zt_ref[...], axis=0, keepdims=True), axis=1, keepdims=True)
+    loss_ref[...] = jnp.broadcast_to(total / toks, loss_ref.shape)
 
     def turn(i, carry):
         tok = pl.ds(pl.multiple_of(i * TCH, TCH), TCH)
@@ -386,6 +390,23 @@
     wait(stores)
 
 
+def finish_kernel(a_hbm, b_hbm, c_hbm, d_hbm, a_out, b_out, c_out, d_out, wide, tall, load_sem, store_sem):
+    loads, stores = [], []
+    for src, buf, dst in ((a_hbm, wide.at[0], a_out), (b_hbm, tall.at[0], b_out), (c_hbm, wide.at[1], c_out), (d_hbm, tall.at[1], d_out)):
+        count = src.shape[0] // 4
+        for first in range(0, src.shape[0], count):
+            at, k = pl.ds(first, count), len(loads)
+            loads.append(pltpu.make_async_copy(src.at[at, :], buf.at[at, :], load_sem.at[k]))
+            stores.append(pltpu.make_async_copy(buf.at[at, :], dst.at[at, :], store_sem.at[k]))
+    for copy in loads:
+        copy.start()
+    for load, store in zip(loads, stores):
+        load.wait()
+        store.start()
+    for copy in stores:
+        copy.wait()
+
+
 def exchange(n, src_ref, all_ref, send_sem, recv_sem):
     me = lax.axis_index("dp")
     barrier = pltpu.get_barrier_semaphore()
@@ -554,24 +575,27 @@
             [(sds(rows_loc, dim), False), (sds(2 * dim, ff), True)],
             [pltpu.VMEM((cap + CH, dim), BF), pltpu.VMEM((8, BLK, dim), F32), pltpu.SMEM((2,), jnp.int32), pltpu.SemaphoreType.DMA((8,))])
 
-        loss = (jnp.sum(stat[0]) - jnp.sum(dht[dim:])) / toks
-        dht, loss = lax.optimization_barrier((dht, loss))
         any_spec = pl.BlockSpec(memory_space=pl.ANY)
-        dw_one, dw_two, dwi_one, dwi_two = pl.pallas_call(
+        *weight_grads, loss = pl.pallas_call(
             functools.partial(query_back_kernel, scale),
-            in_specs=[any_spec] * 5, out_specs=[any_spec] * 4,
-            out_shape=[sds(dim, ff), sds(ff, dim), sds(dim, ff), sds(ff, dim)],
-            scratch_shapes=[
+            in_specs=[pl.BlockSpec(memory_space=pltpu.VMEM)] + [any_spec] * 5, out_specs=[any_spec] * 4 + [pl.BlockSpec(memory_space=pltpu.VMEM)],
+            out_shape=[sds(dim, ff), sds(ff, dim), sds(dim, ff), sds(ff, dim), sds(8, 128)],
+            scratch_shapes=[pltpu.VMEM((8, toks), F32),
                 pltpu.VMEM((dim, ff), F32), pltpu.VMEM((dim, ff), F32), pltpu.VMEM((2 * dim, ff), F32), pltpu.VMEM((2, ff, dim), F32),
                 pltpu.VMEM((toks, dim), BF), pltpu.VMEM((dim, toks), BF), pltpu.VMEM((dim, toks), F32), pltpu.VMEM((dim, toks), BF),
                 pltpu.VMEM((toks, dim), BF), pltpu.VMEM((dim, ff), BF), pltpu.VMEM((ff, dim), BF),
                 pltpu.VMEM((2, dim // 2, ff), F32), pltpu.VMEM((2, dim // 2, ff), F32),
                 pltpu.VMEM((2, 2, dim // 8, ff), F32), pltpu.VMEM((2, 2, dim // 16, ff), F32),
-                pltpu.SemaphoreType.DMA((6,)), pltpu.SemaphoreType.DMA((4,)), pltpu.SemaphoreType.DMA((26,)), pltpu.SemaphoreType.DMA((26,))],
+                pltpu.SemaphoreType.DMA((7,)), pltpu.SemaphoreType.DMA((4,)), pltpu.SemaphoreType.DMA((26,)), pltpu.SemaphoreType.DMA((26,))],
             compiler_params=pltpu.CompilerParams(vmem_limit_bytes=VMEM_LIMIT, collective_id=2, has_side_effects=True),
             cost_estimate=cost(8 * toks * dim * ff), name="query_back",
-        )(x_all, dht, w_one, w_two, dwi_part)
-
-        return loss, d_table, dw_one, dw_two, dwi_one, dwi_two
+        )(stat, x_all, dht, w_one, w_two, dwi_part)
+        weight_grads = pl.pallas_call(
+            finish_kernel, in_specs=[any_spec] * 4, out_specs=[any_spec] * 4, out_shape=[sds(*a.shape) for a in weight_grads],
+            scratch_shapes=[pltpu.VMEM((2, dim, ff), F32), pltpu.VMEM((2, ff, dim), F32), pltpu.SemaphoreType.DMA((16,)), pltpu.SemaphoreType.DMA((16,))],
+            compiler_params=pltpu.CompilerParams(vmem_limit_bytes=VMEM_LIMIT), name="finish",
+        )(*weight_grads)
+
+        return (loss[0, 0], d_table, *weight_grads)
 
     return jax.shard_map(local_step, mesh=mesh, in_specs=(P("dp", None), P(), P(), P(), P(), P("dp", None), P(), P(), P("dp")), out_specs=(P(), P("dp", None), P(), P(), P(), P()), check_vma=False)

time: 329 us -> 320 us (0.973)
  local copies, waits for them, and re-layouts: 15 us -> 1.88 us
  Pallas kernels: 277 us -> 286 us
    unnamed x20 -> x10, local copies, waits for them, and re-layouts: 14.3 us -> 0.03 us
    pallas_call x1 -> x2, Pallas kernels: 81.5 us -> 95.1 us  [the longest x1 83.2 us: local_step(): pl.pallas_call(functools.partial(query_back_kernel, scale), in_specs=[pl....]
    pallas_call x3, Pallas kernels: 160 us -> 156 us  [call(): pl.pallas_call(kernel, in_specs=[spec(None)] + [spec(p) for _, p in ins],...]
where the time goes in v4:
time: 320 us
  Pallas kernels  286 us (89%)
  other arithmetic  16 us (5%)
  between operations  14.6 us (5%)
    pallas_call x3, Pallas kernels, call(): pl.pallas_call(kernel, in_specs=[spec(None)] + [spec(p) for _, p in ins],...  156 us
    pallas_call x1, Pallas kernels, local_step(): pl.pallas_call(functools.partial(query_back_kernel, scale), in_specs=[pl....  83.2 us
    pallas_call x1, Pallas kernels, local_step(): pl.pallas_call(gather_kernel, grid_spec=pltpu.PrefetchScalarGridSpec(num_...  20.1 us
    pallas_call x2, Pallas kernels, share(): pl.pallas_call(functools.partial(kernel, n), out_shape=out, in_specs=[spe...  14.5 us
    pallas_call x1, Pallas kernels, local_step(): pl.pallas_call(finish_kernel, in_specs=[any_spec] * 4, out_specs=[any_spe...  12 us
    sort x1, other arithmetic, local_step(): key_s, offs_s = lax.sort((key, offs), num_keys=1, is_stable=False)  8.22 us
  transfers between devices with their start and end apart: 3, of which 0 were waited for; matrix products, arithmetic and copies ran while one was open for 4% of the time, Pallas kernels for 45%

profile of v4, /device:TPU:0, one launch (start us, length us, event | category | flops | bytes accessed | tf_op | source)
XLA Modules:
  0.0 319.7 jit_solution(12439168381095266735)
XLA Ops:
  7.2 0.0 copy-start.1
  7.2 0.0 copy-start.4
  7.2 0.0 copy-start
  7.2 0.0 copy-start.2
  7.2 0.0 all-gather.3.cloned.1.call-start
  7.3 3.2 compare_reduce_fusion
  10.4 1.2 convert_add_fusion
  11.7 8.2 %shard_map.145 = (s32[8,1,256]{2,1,0:T(1,128)}, bf16[256,512]{1,0:T(8,128)(2,1)}) custom-call(s32[1,256]{1,0:T(1,128)} %bitcast.19, bf16[256,512]{1,0:T(8,128)(2,1)} %x_hbm.1, bf16[512,2048]{1,0:T(8,128)(2,1)} %w1_hbm.3, bf16[2048,512]{1,0:T(8,128)(2,1)} %w2_hbm.3), custom_call_target="tpu_custom_call" | custom-call | tf_op jit(solution)/shard_map/pallas_call | solution.py:462
  19.9 0.0 all-gather.3.cloned.1.call-update
  19.9 0.0 all-gather.5.cloned.1.call-start
  20.0 0.7 all-gather.5.cloned.1.call-update
  20.7 0.2 all-reduce.4.cloned.1.call-start
  20.9 0.0 copy-done.2
  20.9 1.3 and_convert_fusion
  22.2 0.0 copy-done.1
  22.3 0.0 copy-done
  22.3 8.2 %sort.15 = (s32[18432]{0:T(1024)S(1)}, f32[18432]{0:T(1024)S(1)}) sort(s32[18432]{0:T(1024)S(1)} %add_select_fusion, f32[18432]{0:T(1024)S(1)} %concatenate.17), dimensions={0}, to_apply=%region_2.3 | sort | flops 276480 | bytes 294912 | tf_op jit(solution)/shard_map/sort | solution.py:523
  30.5 0.1 slice_compare_fusion
  30.6 0.1 convert_select_fusion
  30.7 0.2 select_maximum_fusion
  30.9 0.9 convert_reduce_fusion.starts_ref
  31.7 0.0 copy-start.3
  31.7 0.6 slice.12
  33.0 0.0 copy-done.4
  33.0 0.1 broadcast_in_dim.40
  33.0 0.9 maximum_bitcast_fusion.attr_ref.attr_hbm
  33.9 0.0 copy-done.3
  33.9 20.1 %gather.1.rows_hbm = bf16[18432,512]{1,0:T(8,128)(2,1)} custom-call(s32[65]{0:T(128)} %copy-done.3, s32[1]{0:T(128)} %bitcast.3.nch_ref, bf16[32768,512]{1,0:T(8,128)(2,1)} %tbl_ref.1, f32[148,8,128]{2,1,0:T(8,128)} %maximum_bitcast_fusion.attr_ref.attr_hbm), custom_call_target="tpu_custom_call" | custom-call | flops 8589934592 | bytes 67108864 | tf_op jit(solution)/shard_map/gather/pallas_call | solution.py:536
  54.1 0.0 all-gather.3.cloned.1.call-done.h_ref
  54.1 48.9 %fwd.1 = (bf16[18432,512]{1,0:T(8,128)(2,1)}, f32[18432,2048]{1,0:T(8,128)}, f32[18432,2048]{1,0:T(8,128)}, f32[2,2048]{1,0:T(2,128)}) custom-call(s32[1]{0:T(128)} %bitcast.3.nch_ref, f32[1,2048]{1,0:T(1,128)} %bitcast.15, bf16[2048,512]{1,0:T(8,128)(2,1)} %all-gather.3.cloned.1.call-done.h_ref, bf16[512,2048]{1,0:T(8,128)(2,1)} %w1_ref.3, ...), custom_call_target="tpu_custom_call" | custom-call | flops 28991029248 | bytes 67108864 | tf_op jit(solution)/shard_map/fwd/pallas_call | solution.py:548
  102.9 0.0 all-gather.5.cloned.1.call-done.x_hbm
  102.9 6.3 %shard_map.146.stat_ref = f32[3,2048]{1,0:T(4,128)} custom-call(f32[2,2048]{1,0:T(2,128)} %get-tuple-element.34.stat_ref, f32[1,2048]{1,0:T(1,128)} %bitcast.18), custom_call_target="tpu_custom_call" | custom-call | tf_op jit(solution)/shard_map/pallas_call | solution.py:462
  109.2 32.0 %logit_back.1 = (bf16[18432,512]{1,0:T(8,128)(2,1)}, f32[520,2048]{1,0:T(8,128)}) custom-call(s32[1]{0:T(128)} %bitcast.3.nch_ref, f32[1,2048]{1,0:T(1,128)} %bitcast.16, f32[3,2048]{1,0:T(4,128)} %shard_map.146.stat_ref, bf16[2048,512]{1,0:T(8,128)(2,1)} %all-gather.3.cloned.1.call-done.h_ref, f32[18432,2048]{1,0:T(8,128)} %get-tuple-element.36.z_hbm, ...), custom_call_target="tpu_custom_call" | custom-call | flops 19327352832 | bytes 67108864 | tf_op jit(solution)/shard_map/logit_back/pallas_call | solution.py:548
  141.2 0.0 all-reduce.4.cloned.1.call-update
  141.2 75.5 %tower_back.1 = (f32[32768,512]{1,0:T(8,128)}, f32[1024,2048]{1,0:T(8,128)}) custom-call(s32[1]{0:T(128)} %bitcast.3.nch_ref, s32[65]{0:T(128)} %copy-done.3, bf16[512,2048]{1,0:T(8,128)(2,1)} %w1_ref.3, bf16[2048,512]{1,0:T(8,128)(2,1)} %w2_ref.3, f32[148,8,128]{2,1,0:T(8,128)} %maximum_bitcast_fusion.attr_ref.attr_hbm, ...), custom_call_target="tpu_custom_call" | custom-call | flops 38654705664 | bytes 67108864 | tf_op jit(solution)/shard_map/tower_back/pallas_call | solution.py:548
  216.7 0.0 all-reduce.4.cloned.1.call-done.dht_hbm
  216.8 83.2 %query_back.1 = (f32[512,2048]{1,0:T(8,128)}, f32[2048,512]{1,0:T(8,128)}, f32[512,2048]{1,0:T(8,128)}, f32[2048,512]{1,0:T(8,128)}, f32[8,128]{1,0:T(8,128)}) custom-call(f32[3,2048]{1,0:T(4,128)} %shard_map.146.stat_ref, bf16[2048,512]{1,0:T(8,128)(2,1)} %all-gather.5.cloned.1.call-done.x_hbm, f32[520,2048]{1,0:T(8,128)} %all-reduce.4.cloned.1.call-done.dht_hbm, ...), custom_call_target="tpu_custom_call" | custom-call | flops 17179869184 | bytes 67108864 | tf_op jit(solution)/shard_map/query_back/pallas_call | solution.py:579
  299.9 1.2 slice.15
  301.1 12.0 %finish.1 = (f32[512,2048]{1,0:T(8,128)}, f32[2048,512]{1,0:T(8,128)}, f32[512,2048]{1,0:T(8,128)}, f32[2048,512]{1,0:T(8,128)}) custom-call(f32[512,2048]{1,0:T(8,128)} %get-tuple-element.44.a_hbm, f32[2048,512]{1,0:T(8,128)} %get-tuple-element.45.b_hbm, f32[512,2048]{1,0:T(8,128)} %get-tuple-element.46.c_hbm, f32[2048,512]{1,0:T(8,128)} %get-tuple-element.47.d_hbm), custom_call_target="tpu_custom_call" | custom-call | tf_op jit(solution)/shard_map/finish/pallas_call | solution.py:593
  (3 shorter events, 0.0 us)
Async XLA Ops:
  7.2 15.1 %copy-start.1 = (s32[18432]{0:T(1024)S(1)}, s32[18432]{0:T(1024)}, u32[]{:S(2)}) copy-start(s32[18432]{0:T(1024)} %constant.10.clone.1) | copy-start | bytes 221188
  7.2 25.8 %copy-start.4 = (f32[8]{0:T(128)S(1)}, f32[8]{0:T(128)}, u32[]{:S(2)}) copy-start(f32[8]{0:T(128)} %constant.50.clone) | copy-start | bytes 100
  7.2 15.1 %copy-start = (s32[16384]{0:T(1024)S(1)}, s32[16384]{0:T(1024)}, u32[]{:S(2)}) copy-start(s32[16384]{0:T(1024)} %param.16) | copy-start | bytes 196612
  7.2 13.7 %copy-start.2 = (f32[16384]{0:T(1024)S(1)}, f32[16384]{0:T(1024)}, u32[]{:S(2)}) copy-start(f32[16384]{0:T(1024)} %param.17) | copy-start | bytes 196612
  7.2 46.9 %all-gather.3.cloned.1.call-start = ((), (), s32[]{:S(2)}) async-start(), calls=%async_computation | async-start | bytes 2359296 | tf_op jit(solution)/shard_map/all_gather | solution.py:513
  19.9 83.0 %all-gather.5.cloned.1.call-start = ((), (), s32[]{:S(2)}) async-start(), calls=%async_computation.1 | async-start | bytes 2359296 | tf_op jit(solution)/shard_map/all_gather | solution.py:514
  20.7 196.1 %all-reduce.4.cloned.1.call-start = ((), (), s32[]{:S(2)}) async-start(), calls=%async_computation.2 | async-start | bytes 8519680 | tf_op jit(solution)/shard_map/psum | solution.py:571
  31.7 2.2 copy-start.3
Sparse Core Ops, SparseCore 0:
  20.0 22.8 all-gather.2
  44.7 21.9 all-gather.4
  141.4 68.8 all-reduce.3

commit v5 on v4

--- a/solution.py
+++ b/solution.py
@@ -15,8 +15,9 @@
 BLK = 512
 TCH = 512
 SUB = 8
-PAIR = 2
-GROUP = 4
+PAIR = 4
+GROUP = 8
+RING = 12
 WIN = 128
 FB = 256
 FWD_FB = 512
@@ -390,7 +391,7 @@
     wait(stores)
 
 
-def finish_kernel(a_hbm, b_hbm, c_hbm, d_hbm, a_out, b_out, c_out, d_out, wide, tall, load_sem, store_sem):
+def finish_kernel(loss_ref, a_hbm, b_hbm, c_hbm, d_hbm, loss_out, a_out, b_out, c_out, d_out, wide, tall, load_sem, store_sem):
     loads, stores = [], []
     for src, buf, dst in ((a_hbm, wide.at[0], a_out), (b_hbm, tall.at[0], b_out), (c_hbm, wide.at[1], c_out), (d_hbm, tall.at[1], d_out)):
         count = src.shape[0] // 4
@@ -400,6 +401,7 @@
             stores.append(pltpu.make_async_copy(buf.at[at, :], dst.at[at, :], store_sem.at[k]))
     for copy in loads:
         copy.start()
+    loss_out[...] = loss_ref[0:1, 0:1]
     for load, store in zip(loads, stores):
         load.wait()
         store.start()
@@ -573,7 +575,7 @@
             tower_back_kernel, "tower_back", 8 * cap * dim * ff // 4,
             [(starts, None), (wi_one, True), (wi_two, True), (attr, True), (g, False), (rows, False), (pre, False)],
             [(sds(rows_loc, dim), False), (sds(2 * dim, ff), True)],
-            [pltpu.VMEM((cap + CH, dim), BF), pltpu.VMEM((8, BLK, dim), F32), pltpu.SMEM((2,), jnp.int32), pltpu.SemaphoreType.DMA((8,))])
+            [pltpu.VMEM((cap + CH, dim), BF), pltpu.VMEM((RING, BLK, dim), F32), pltpu.SMEM((2,), jnp.int32), pltpu.SemaphoreType.DMA((RING,))])
 
         any_spec = pl.BlockSpec(memory_space=pl.ANY)
         *weight_grads, loss = pl.pallas_call(
@@ -590,12 +592,14 @@
             compiler_params=pltpu.CompilerParams(vmem_limit_bytes=VMEM_LIMIT, collective_id=2, has_side_effects=True),
             cost_estimate=cost(8 * toks * dim * ff), name="query_back",
         )(stat, x_all, dht, w_one, w_two, dwi_part)
-        weight_grads = pl.pallas_call(
-            finish_kernel, in_specs=[any_spec] * 4, out_specs=[any_spec] * 4, out_shape=[sds(*a.shape) for a in weight_grads],
+        vmem_spec = pl.BlockSpec(memory_space=pltpu.VMEM)
+        loss, *weight_grads = pl.pallas_call(
+            finish_kernel, in_specs=[vmem_spec] + [any_spec] * 4, out_specs=[vmem_spec] + [any_spec] * 4,
+            out_shape=[sds(1, 1)] + [sds(*a.shape) for a in weight_grads],
             scratch_shapes=[pltpu.VMEM((2, dim, ff), F32), pltpu.VMEM((2, ff, dim), F32), pltpu.SemaphoreType.DMA((16,)), pltpu.SemaphoreType.DMA((16,))],
             compiler_params=pltpu.CompilerParams(vmem_limit_bytes=VMEM_LIMIT), name="finish",
-        )(*weight_grads)
-
-        return (loss[0, 0], d_table, *weight_grads)
+        )(loss, *weight_grads)
+
+        return (loss.reshape(()), d_table, *weight_grads)
 
     return jax.shard_map(local_step, mesh=mesh, in_specs=(P("dp", None), P(), P(), P(), P(), P("dp", None), P(), P(), P("dp")), out_specs=(P(), P("dp", None), P(), P(), P(), P()), check_vma=False)

time: 320 us -> 322 us (level); the launches traced: 320 us -> 318 us
  no operation moved by 1% of the time
where the time goes in v5:
time: 322 us; the launch traced here: 318 us
  Pallas kernels  285 us (89%)
  other arithmetic  16 us (5%)
  between operations  15 us (5%)
    pallas_call x3, Pallas kernels, call(): pl.pallas_call(kernel, in_specs=[spec(None)] + [spec(p) for _, p in ins],...  155 us
    pallas_call x1, Pallas kernels, local_step(): pl.pallas_call(functools.partial(query_back_kernel, scale), in_specs=[pl....  83 us
    pallas_call x1, Pallas kernels, local_step(): pl.pallas_call(gather_kernel, grid_spec=pltpu.PrefetchScalarGridSpec(num_...  19.5 us
    pallas_call x2, Pallas kernels, share(): pl.pallas_call(functools.partial(kernel, n), out_shape=out, in_specs=[spe...  14.5 us
    pallas_call x1, Pallas kernels, local_step(): pl.pallas_call(finish_kernel, in_specs=[vmem_spec] + [any_spec] * 4, out_...  13.2 us
    sort x1, other arithmetic, local_step(): key_s, offs_s = lax.sort((key, offs), num_keys=1, is_stable=False)  8.22 us
  transfers between devices with their start and end apart: 3, of which 0 were waited for; matrix products, arithmetic and copies ran while one was open for 4% of the time, Pallas kernels for 45%

profile of v5, /device:TPU:0, one launch (start us, length us, event | category | flops | bytes accessed | tf_op | source)
XLA Modules:
  0.0 318.2 jit_solution(4251979842218012548)
XLA Ops:
  7.2 0.0 copy-start.1
  7.2 0.0 copy-start.4
  7.2 0.0 copy-start
  7.2 0.0 copy-start.2
  7.2 0.0 all-gather.3.cloned.1.call-start
  7.3 3.2 compare_reduce_fusion
  10.4 1.2 convert_add_fusion
  11.7 8.2 %shard_map.145 = (s32[8,1,256]{2,1,0:T(1,128)}, bf16[256,512]{1,0:T(8,128)(2,1)}) custom-call(s32[1,256]{1,0:T(1,128)} %bitcast.19, bf16[256,512]{1,0:T(8,128)(2,1)} %x_hbm.1, bf16[512,2048]{1,0:T(8,128)(2,1)} %w1_hbm.3, bf16[2048,512]{1,0:T(8,128)(2,1)} %w2_hbm.3), custom_call_target="tpu_custom_call" | custom-call | tf_op jit(solution)/shard_map/pallas_call | solution.py:464
  19.9 0.0 all-gather.3.cloned.1.call-update
  19.9 0.0 all-gather.5.cloned.1.call-start
  20.0 0.7 all-gather.5.cloned.1.call-update
  20.7 0.2 all-reduce.4.cloned.1.call-start
  20.9 0.0 copy-done.2
  20.9 1.3 and_convert_fusion
  22.2 0.0 copy-done.1
  22.2 0.0 copy-done
  22.3 8.2 %sort.15 = (s32[18432]{0:T(1024)S(1)}, f32[18432]{0:T(1024)S(1)}) sort(s32[18432]{0:T(1024)S(1)} %add_select_fusion, f32[18432]{0:T(1024)S(1)} %concatenate.17), dimensions={0}, to_apply=%region_2.3 | sort | flops 276480 | bytes 294912 | tf_op jit(solution)/shard_map/sort | solution.py:525
  30.5 0.1 slice_compare_fusion
  30.6 0.1 convert_select_fusion
  30.7 0.2 select_maximum_fusion
  30.8 0.9 convert_reduce_fusion.starts_ref
  31.7 0.0 copy-start.3
  31.7 0.6 slice.9
  33.0 0.0 copy-done.4
  33.0 0.1 broadcast_in_dim.40
  33.0 0.9 maximum_bitcast_fusion.attr_ref.attr_hbm
  33.9 0.0 copy-done.3
  33.9 19.5 %gather.1.rows_hbm = bf16[18432,512]{1,0:T(8,128)(2,1)} custom-call(s32[65]{0:T(128)} %copy-done.3, s32[1]{0:T(128)} %bitcast.3.nch_ref, bf16[32768,512]{1,0:T(8,128)(2,1)} %tbl_ref.1, f32[148,8,128]{2,1,0:T(8,128)} %maximum_bitcast_fusion.attr_ref.attr_hbm), custom_call_target="tpu_custom_call" | custom-call | flops 8589934592 | bytes 67108864 | tf_op jit(solution)/shard_map/gather/pallas_call | solution.py:538
  53.4 0.0 all-gather.3.cloned.1.call-done.h_ref
  53.4 49.0 %fwd.1 = (bf16[18432,512]{1,0:T(8,128)(2,1)}, f32[18432,2048]{1,0:T(8,128)}, f32[18432,2048]{1,0:T(8,128)}, f32[2,2048]{1,0:T(2,128)}) custom-call(s32[1]{0:T(128)} %bitcast.3.nch_ref, f32[1,2048]{1,0:T(1,128)} %bitcast.15, bf16[2048,512]{1,0:T(8,128)(2,1)} %all-gather.3.cloned.1.call-done.h_ref, bf16[512,2048]{1,0:T(8,128)(2,1)} %w1_ref.3, ...), custom_call_target="tpu_custom_call" | custom-call | flops 28991029248 | bytes 67108864 | tf_op jit(solution)/shard_map/fwd/pallas_call | solution.py:550
  102.5 0.0 all-gather.5.cloned.1.call-done.x_hbm
  102.5 6.3 %shard_map.146.stat_ref = f32[3,2048]{1,0:T(4,128)} custom-call(f32[2,2048]{1,0:T(2,128)} %get-tuple-element.35.stat_ref, f32[1,2048]{1,0:T(1,128)} %bitcast.18), custom_call_target="tpu_custom_call" | custom-call | tf_op jit(solution)/shard_map/pallas_call | solution.py:464
  108.8 32.0 %logit_back.1 = (bf16[18432,512]{1,0:T(8,128)(2,1)}, f32[520,2048]{1,0:T(8,128)}) custom-call(s32[1]{0:T(128)} %bitcast.3.nch_ref, f32[1,2048]{1,0:T(1,128)} %bitcast.16, f32[3,2048]{1,0:T(4,128)} %shard_map.146.stat_ref, bf16[2048,512]{1,0:T(8,128)(2,1)} %all-gather.3.cloned.1.call-done.h_ref, f32[18432,2048]{1,0:T(8,128)} %get-tuple-element.37.z_hbm, ...), custom_call_target="tpu_custom_call" | custom-call | flops 19327352832 | bytes 67108864 | tf_op jit(solution)/shard_map/logit_back/pallas_call | solution.py:550
  140.8 0.0 all-reduce.4.cloned.1.call-update
  140.8 74.3 %tower_back.1 = (f32[32768,512]{1,0:T(8,128)}, f32[1024,2048]{1,0:T(8,128)}) custom-call(s32[1]{0:T(128)} %bitcast.3.nch_ref, s32[65]{0:T(128)} %copy-done.3, bf16[512,2048]{1,0:T(8,128)(2,1)} %w1_ref.3, bf16[2048,512]{1,0:T(8,128)(2,1)} %w2_ref.3, f32[148,8,128]{2,1,0:T(8,128)} %maximum_bitcast_fusion.attr_ref.attr_hbm, ...), custom_call_target="tpu_custom_call" | custom-call | flops 38654705664 | bytes 67108864 | tf_op jit(solution)/shard_map/tower_back/pallas_call | solution.py:550
  215.1 0.0 all-reduce.4.cloned.1.call-done.dht_hbm
  215.1 83.0 %query_back.1 = (f32[512,2048]{1,0:T(8,128)}, f32[2048,512]{1,0:T(8,128)}, f32[512,2048]{1,0:T(8,128)}, f32[2048,512]{1,0:T(8,128)}, f32[8,128]{1,0:T(8,128)}) custom-call(f32[3,2048]{1,0:T(4,128)} %shard_map.146.stat_ref, bf16[2048,512]{1,0:T(8,128)(2,1)} %all-gather.5.cloned.1.call-done.x_hbm, f32[520,2048]{1,0:T(8,128)} %all-reduce.4.cloned.1.call-done.dht_hbm, ...), custom_call_target="tpu_custom_call" | custom-call | flops 17179869184 | bytes 67108864 | tf_op jit(solution)/shard_map/query_back/pallas_call | solution.py:581
  298.1 13.2 %finish.1 = (f32[1,1]{1,0:T(1,128)}, f32[512,2048]{1,0:T(8,128)}, f32[2048,512]{1,0:T(8,128)}, f32[512,2048]{1,0:T(8,128)}, f32[2048,512]{1,0:T(8,128)}) custom-call(f32[8,128]{1,0:T(8,128)} %get-tuple-element.43.loss_ref, f32[512,2048]{1,0:T(8,128)} %get-tuple-element.44.a_hbm, f32[2048,512]{1,0:T(8,128)} %get-tuple-element.45.b_hbm, ...), custom_call_target="tpu_custom_call" | custom-call | tf_op jit(solution)/shard_map/finish/pallas_call | solution.py:596
  (3 shorter events, 0.0 us)
Async XLA Ops:
  7.2 15.1 %copy-start.1 = (s32[18432]{0:T(1024)S(1)}, s32[18432]{0:T(1024)}, u32[]{:S(2)}) copy-start(s32[18432]{0:T(1024)} %constant.10.clone.1) | copy-start | bytes 221188
  7.2 25.8 %copy-start.4 = (f32[8]{0:T(128)S(1)}, f32[8]{0:T(128)}, u32[]{:S(2)}) copy-start(f32[8]{0:T(128)} %constant.50.clone) | copy-start | bytes 100
  7.2 15.1 %copy-start = (s32[16384]{0:T(1024)S(1)}, s32[16384]{0:T(1024)}, u32[]{:S(2)}) copy-start(s32[16384]{0:T(1024)} %param.16) | copy-start | bytes 196612
  7.2 13.7 %copy-start.2 = (f32[16384]{0:T(1024)S(1)}, f32[16384]{0:T(1024)}, u32[]{:S(2)}) copy-start(f32[16384]{0:T(1024)} %param.17) | copy-start | bytes 196612
  7.2 46.2 %all-gather.3.cloned.1.call-start = ((), (), s32[]{:S(2)}) async-start(), calls=%async_computation | async-start | bytes 2359296 | tf_op jit(solution)/shard_map/all_gather | solution.py:515
  19.9 82.6 %all-gather.5.cloned.1.call-start = ((), (), s32[]{:S(2)}) async-start(), calls=%async_computation.1 | async-start | bytes 2359296 | tf_op jit(solution)/shard_map/all_gather | solution.py:516
  20.7 194.4 %all-reduce.4.cloned.1.call-start = ((), (), s32[]{:S(2)}) async-start(), calls=%async_computation.2 | async-start | bytes 8519680 | tf_op jit(solution)/shard_map/psum | solution.py:573
  31.7 2.2 copy-start.3
Sparse Core Ops, SparseCore 0:
  20.0 22.8 all-gather.2
  44.7 21.9 all-gather.4
  140.9 68.8 all-reduce.3

commit v6 on v5

--- a/solution.py
+++ b/solution.py
@@ -16,7 +16,7 @@
 TCH = 512
 SUB = 8
 PAIR = 4
-GROUP = 8
+GROUP = 4
 RING = 12
 WIN = 128
 FB = 256
@@ -355,16 +355,14 @@
     wait(step[1])
     step[1] = stage1(1)
     lax.fori_loop(0, toks // TCH, turn, 0)
-    lax.fori_loop(0, units // 4, unit, 0)
+    lax.fori_loop(0, units // 2, unit, 0)
     wait(step[0])
     step[0] = stage2(0)
-    lax.fori_loop(units // 4, units // 2, unit, 0)
     wait(step[1])
     step[1] = stage2(1)
-    lax.fori_loop(units // 2, units * 5 // 8, unit, 0)
+    lax.fori_loop(units // 2, units * 3 // 4, unit, 0)
     wait(step[0])
     step[0] = stage3(0)
-    lax.fori_loop(units * 5 // 8, units * 3 // 4, unit, 0)
     wait(step[1])
     step[1] = stage3(1)
     lax.fori_loop(units * 3 // 4, units, unit, 0)

time: 322 us -> 319 us (level)
  no operation moved by 1% of the time
where the time goes in v6:
time: 319 us; the launch traced here: 318 us
  Pallas kernels  286 us (90%)
  other arithmetic  16 us (5%)
  between operations  14.6 us (5%)
    pallas_call x3, Pallas kernels, call(): pl.pallas_call(kernel, in_specs=[spec(None)] + [spec(p) for _, p in ins],...  155 us
    pallas_call x1, Pallas kernels, local_step(): pl.pallas_call(functools.partial(query_back_kernel, scale), in_specs=[pl....  83.5 us
    pallas_call x1, Pallas kernels, local_step(): pl.pallas_call(gather_kernel, grid_spec=pltpu.PrefetchScalarGridSpec(num_...  20.1 us
    pallas_call x2, Pallas kernels, share(): pl.pallas_call(functools.partial(kernel, n), out_shape=out, in_specs=[spe...  14.5 us
    pallas_call x1, Pallas kernels, local_step(): pl.pallas_call(finish_kernel, in_specs=[vmem_spec] + [any_spec] * 4, out_...  13.2 us
    sort x1, other arithmetic, local_step(): key_s, offs_s = lax.sort((key, offs), num_keys=1, is_stable=False)  8.22 us
  transfers between devices with their start and end apart: 3, of which 0 were waited for; matrix products, arithmetic and copies ran while one was open for 4% of the time, Pallas kernels for 45%

profile of v6, /device:TPU:0, one launch (start us, length us, event | category | flops | bytes accessed | tf_op | source)
XLA Modules:
  0.0 318.3 jit_solution(8771250364026903355)
XLA Ops:
  7.2 0.0 copy-start.1
  7.2 0.0 copy-start.4
  7.2 0.0 copy-start
  7.2 0.0 copy-start.2
  7.2 0.0 all-gather.3.cloned.1.call-start
  7.3 3.2 compare_reduce_fusion
  10.4 1.2 convert_add_fusion
  11.7 8.2 %shard_map.145 = (s32[8,1,256]{2,1,0:T(1,128)}, bf16[256,512]{1,0:T(8,128)(2,1)}) custom-call(s32[1,256]{1,0:T(1,128)} %bitcast.19, bf16[256,512]{1,0:T(8,128)(2,1)} %x_hbm.1, bf16[512,2048]{1,0:T(8,128)(2,1)} %w1_hbm.3, bf16[2048,512]{1,0:T(8,128)(2,1)} %w2_hbm.3), custom_call_target="tpu_custom_call" | custom-call | tf_op jit(solution)/shard_map/pallas_call | solution.py:462
  19.9 0.0 all-gather.3.cloned.1.call-update
  19.9 0.0 all-gather.5.cloned.1.call-start
  20.0 0.7 all-gather.5.cloned.1.call-update
  20.7 0.2 all-reduce.4.cloned.1.call-start
  20.9 0.0 copy-done.2
  20.9 1.3 and_convert_fusion
  22.2 0.0 copy-done.1
  22.3 0.0 copy-done
  22.3 8.2 %sort.15 = (s32[18432]{0:T(1024)S(1)}, f32[18432]{0:T(1024)S(1)}) sort(s32[18432]{0:T(1024)S(1)} %add_select_fusion, f32[18432]{0:T(1024)S(1)} %concatenate.17), dimensions={0}, to_apply=%region_2.3 | sort | flops 276480 | bytes 294912 | tf_op jit(solution)/shard_map/sort | solution.py:523
  30.5 0.1 slice_compare_fusion
  30.6 0.1 convert_select_fusion
  30.7 0.2 select_maximum_fusion
  30.9 0.9 convert_reduce_fusion.starts_ref
  31.7 0.0 copy-start.3
  31.7 0.6 slice.9
  33.0 0.0 copy-done.4
  33.0 0.1 broadcast_in_dim.40
  33.0 0.9 maximum_bitcast_fusion.attr_ref.attr_hbm
  33.9 0.0 copy-done.3
  33.9 20.1 %gather.1.rows_hbm = bf16[18432,512]{1,0:T(8,128)(2,1)} custom-call(s32[65]{0:T(128)} %copy-done.3, s32[1]{0:T(128)} %bitcast.3.nch_ref, bf16[32768,512]{1,0:T(8,128)(2,1)} %tbl_ref.1, f32[148,8,128]{2,1,0:T(8,128)} %maximum_bitcast_fusion.attr_ref.attr_hbm), custom_call_target="tpu_custom_call" | custom-call | flops 8589934592 | bytes 67108864 | tf_op jit(solution)/shard_map/gather/pallas_call | solution.py:536
  54.1 0.0 all-gather.3.cloned.1.call-done.h_ref
  54.1 48.9 %fwd.1 = (bf16[18432,512]{1,0:T(8,128)(2,1)}, f32[18432,2048]{1,0:T(8,128)}, f32[18432,2048]{1,0:T(8,128)}, f32[2,2048]{1,0:T(2,128)}) custom-call(s32[1]{0:T(128)} %bitcast.3.nch_ref, f32[1,2048]{1,0:T(1,128)} %bitcast.15, bf16[2048,512]{1,0:T(8,128)(2,1)} %all-gather.3.cloned.1.call-done.h_ref, bf16[512,2048]{1,0:T(8,128)(2,1)} %w1_ref.3, ...), custom_call_target="tpu_custom_call" | custom-call | flops 28991029248 | bytes 67108864 | tf_op jit(solution)/shard_map/fwd/pallas_call | solution.py:548
  102.9 0.0 all-gather.5.cloned.1.call-done.x_hbm
  102.9 6.3 %shard_map.146.stat_ref = f32[3,2048]{1,0:T(4,128)} custom-call(f32[2,2048]{1,0:T(2,128)} %get-tuple-element.35.stat_ref, f32[1,2048]{1,0:T(1,128)} %bitcast.18), custom_call_target="tpu_custom_call" | custom-call | tf_op jit(solution)/shard_map/pallas_call | solution.py:462
  109.2 32.0 %logit_back.1 = (bf16[18432,512]{1,0:T(8,128)(2,1)}, f32[520,2048]{1,0:T(8,128)}) custom-call(s32[1]{0:T(128)} %bitcast.3.nch_ref, f32[1,2048]{1,0:T(1,128)} %bitcast.16, f32[3,2048]{1,0:T(4,128)} %shard_map.146.stat_ref, bf16[2048,512]{1,0:T(8,128)(2,1)} %all-gather.3.cloned.1.call-done.h_ref, f32[18432,2048]{1,0:T(8,128)} %get-tuple-element.37.z_hbm, ...), custom_call_target="tpu_custom_call" | custom-call | flops 19327352832 | bytes 67108864 | tf_op jit(solution)/shard_map/logit_back/pallas_call | solution.py:548
  141.2 0.0 all-reduce.4.cloned.1.call-update
  141.2 73.8 %tower_back.1 = (f32[32768,512]{1,0:T(8,128)}, f32[1024,2048]{1,0:T(8,128)}) custom-call(s32[1]{0:T(128)} %bitcast.3.nch_ref, s32[65]{0:T(128)} %copy-done.3, bf16[512,2048]{1,0:T(8,128)(2,1)} %w1_ref.3, bf16[2048,512]{1,0:T(8,128)(2,1)} %w2_ref.3, f32[148,8,128]{2,1,0:T(8,128)} %maximum_bitcast_fusion.attr_ref.attr_hbm, ...), custom_call_target="tpu_custom_call" | custom-call | flops 38654705664 | bytes 67108864 | tf_op jit(solution)/shard_map/tower_back/pallas_call | solution.py:548
  215.1 0.0 all-reduce.4.cloned.1.call-done.dht_hbm
  215.1 83.5 %query_back.1 = (f32[512,2048]{1,0:T(8,128)}, f32[2048,512]{1,0:T(8,128)}, f32[512,2048]{1,0:T(8,128)}, f32[2048,512]{1,0:T(8,128)}, f32[8,128]{1,0:T(8,128)}) custom-call(f32[3,2048]{1,0:T(4,128)} %shard_map.146.stat_ref, bf16[2048,512]{1,0:T(8,128)(2,1)} %all-gather.5.cloned.1.call-done.x_hbm, f32[520,2048]{1,0:T(8,128)} %all-reduce.4.cloned.1.call-done.dht_hbm, ...), custom_call_target="tpu_custom_call" | custom-call | flops 17179869184 | bytes 67108864 | tf_op jit(solution)/shard_map/query_back/pallas_call | solution.py:579
  298.6 13.2 %finish.1 = (f32[1,1]{1,0:T(1,128)}, f32[512,2048]{1,0:T(8,128)}, f32[2048,512]{1,0:T(8,128)}, f32[512,2048]{1,0:T(8,128)}, f32[2048,512]{1,0:T(8,128)}) custom-call(f32[8,128]{1,0:T(8,128)} %get-tuple-element.43.loss_ref, f32[512,2048]{1,0:T(8,128)} %get-tuple-element.44.a_hbm, f32[2048,512]{1,0:T(8,128)} %get-tuple-element.45.b_hbm, ...), custom_call_target="tpu_custom_call" | custom-call | tf_op jit(solution)/shard_map/finish/pallas_call | solution.py:594
  (3 shorter events, 0.0 us)
Async XLA Ops:
  7.2 15.1 %copy-start.1 = (s32[18432]{0:T(1024)S(1)}, s32[18432]{0:T(1024)}, u32[]{:S(2)}) copy-start(s32[18432]{0:T(1024)} %constant.10.clone.1) | copy-start | bytes 221188
  7.2 25.8 %copy-start.4 = (f32[8]{0:T(128)S(1)}, f32[8]{0:T(128)}, u32[]{:S(2)}) copy-start(f32[8]{0:T(128)} %constant.50.clone) | copy-start | bytes 100
  7.2 15.1 %copy-start = (s32[16384]{0:T(1024)S(1)}, s32[16384]{0:T(1024)}, u32[]{:S(2)}) copy-start(s32[16384]{0:T(1024)} %param.16) | copy-start | bytes 196612
  7.2 13.7 %copy-start.2 = (f32[16384]{0:T(1024)S(1)}, f32[16384]{0:T(1024)}, u32[]{:S(2)}) copy-start(f32[16384]{0:T(1024)} %param.17) | copy-start | bytes 196612
  7.2 46.9 %all-gather.3.cloned.1.call-start = ((), (), s32[]{:S(2)}) async-start(), calls=%async_computation | async-start | bytes 2359296 | tf_op jit(solution)/shard_map/all_gather | solution.py:513
  19.9 83.0 %all-gather.5.cloned.1.call-start = ((), (), s32[]{:S(2)}) async-start(), calls=%async_computation.1 | async-start | bytes 2359296 | tf_op jit(solution)/shard_map/all_gather | solution.py:514
  20.7 194.4 %all-reduce.4.cloned.1.call-start = ((), (), s32[]{:S(2)}) async-start(), calls=%async_computation.2 | async-start | bytes 8519680 | tf_op jit(solution)/shard_map/psum | solution.py:571
  31.7 2.2 copy-start.3
Sparse Core Ops, SparseCore 0:
  20.0 22.8 all-gather.2
  44.7 21.9 all-gather.4
  141.4 68.8 all-reduce.3
